TPU v7x, 256 devices: a 4x2x16 block of a 4x16x16 slice. The times are simulated.
256 devices in a mesh: models: 2 (over y), leaf: 128 (over x, z, core).
Axes of the slice: x: 4, y: 2, z: 16, core: 2. Of those that a mesh axis runs over, the one named last changes fastest.
The devices are a block of a 4x16x16 slice.
Arguments:
- slip_rate: float32 [1048576], P(('models', 'leaf')), parts along dimension 0, may hold values from -6 to 6
- near_blocks: bfloat16 [4096, 3, 256, 256], P(('models', 'leaf')), parts along dimension 0, may hold values from -0.21875 to 0.21875
- near_index: int32 [4096, 3], P(('models', 'leaf')), parts along dimension 0, may hold values from 0 to 2047, as said below
- far_left: bfloat16 [11, 32, 1048576], P(None, None, ('models', 'leaf')), parts along dimension 2, may hold values from -1 to 1
- far_right: bfloat16 [11, 32, 1048576], P(None, None, ('models', 'leaf')), parts along dimension 2, may hold values from -6 to 6
- far_ranks: int32 [4096, 11], P(('models', 'leaf')), parts along dimension 0, may hold values from 8 to 32
Outputs:
- first_stress: float32 [1048576], P(('models', 'leaf')), parts along dimension 0
- second_stress: float32 [1048576], P(('models', 'leaf')), parts along dimension 0
There are 2 independent parts, one for each index of `models`. A program takes and returns all parts, laid end to end along the dimension named above; each array names one. Nothing has to cross between parts.
Inputs may be any that keep to these rules, and one draw needn't show every extreme that they name: near_index[i, 0] = i; every other entry is a leaf j != i with |j - i| <= 16, and distance 16 occurs.
All inputs are finite; a program needn't handle non-finite values.
Results may differ from a plain program's by a relative error of at most 0.0045.
Values may be sent and summed in bfloat16 or wider, within the bound.
A program may use at most 64 MiB of HBM per device.

v0:
```python
import math

import jax
import jax.numpy as jnp
from jax import lax
from jax.sharding import PartitionSpec as P


def partner_2(value, axis, stride):
    return lax.ppermute(value, axis, [(i, i ^ 1 << stride) for i in range(lax.axis_size(axis))])


def padded(block, sides, width):
    for axis, dim in sides:
        count = lax.axis_size(axis)
        forward = [(i, i + 1) for i in range(count - 1)]
        backward = [(target, source) for source, target in forward]
        low = lax.ppermute(
            lax.slice_in_dim(block, block.shape[dim] - width, None, axis=dim), axis, forward
        )
        high = lax.ppermute(lax.slice_in_dim(block, 0, width, axis=dim), axis, backward)
        block = jnp.concatenate([low, block, high], axis=dim)
    return block


def far_partners(device_sums, cross_levels):
    outputs = []
    accumulated = device_sums
    for bit_no in range(cross_levels):
        received = partner_2(accumulated, "leaf", bit_no)
        outputs.append(received[bit_no])
        accumulated = accumulated + received
    return outputs


def matvec(operand, near_blocks, near_index, far_left, far_right, far_ranks):
    local_leaves = near_blocks.shape[0]
    leaf_size = near_blocks.shape[2]
    levels = far_left.shape[0]
    rank_cols = far_left.shape[1]
    slip_rows = operand.reshape(local_leaves, leaf_size)
    extended = padded(slip_rows, (("leaf", 0),), local_leaves)
    offset = lax.axis_index("leaf") * local_leaves - local_leaves
    position = near_index - offset
    onehot = (
        position[:, :, None] == jnp.arange(3 * local_leaves, dtype=jnp.int32)[None, None, :]
    ).astype(jnp.bfloat16)
    picked = jnp.einsum("ikj,jp->ikp", onehot, extended, preferred_element_type=jnp.float32).astype(
        jnp.bfloat16
    )
    result = jnp.einsum("ikpq,ikq->ip", near_blocks, picked, preferred_element_type=jnp.float32)
    right_part = far_right.reshape(levels, rank_cols, local_leaves, leaf_size)
    projected = jnp.einsum(
        "lrcp,cp->lcr", right_part, slip_rows, preferred_element_type=jnp.float32
    )
    local_levels = local_leaves.bit_length() - 1
    cross_levels = levels - local_levels
    columns = []
    for level_no in range(local_levels):
        span_size = 2**level_no
        cluster_sums = (
            projected[level_no].reshape(local_leaves // span_size, span_size, rank_cols).sum(axis=1)
        )
        cluster_sums = cluster_sums * (1.0 / math.sqrt(leaf_size * span_size))
        partner = cluster_sums.reshape(-1, 2, rank_cols)[:, ::-1, :].reshape(-1, rank_cols)
        columns.append(jnp.repeat(partner, span_size, axis=0))
    device_sums = jnp.sum(projected[local_levels:], axis=1)
    partner_list = far_partners(device_sums, cross_levels)
    for bit_no in range(cross_levels):
        scale = 1.0 / math.sqrt(leaf_size * 2 ** (local_levels + bit_no))
        columns.append(
            jnp.broadcast_to(partner_list[bit_no][None, :] * scale, (local_leaves, rank_cols))
        )
    stacked = jnp.stack(columns)
    rank_mask = (
        jnp.arange(rank_cols, dtype=jnp.int32)[None, None, :] < jnp.transpose(far_ranks)[:, :, None]
    )
    weights = jnp.where(rank_mask, stacked, 0.0).astype(jnp.bfloat16)
    left_part = far_left.reshape(levels, rank_cols, local_leaves, leaf_size)
    result = result + jnp.einsum(
        "lrcp,lcr->cp", left_part, weights, preferred_element_type=jnp.float32
    )
    return result.reshape(-1)


def local(slip_rate, near_blocks, near_index, far_left, far_right, far_ranks):
    slip_bf = slip_rate.astype(jnp.bfloat16)
    first_stress = matvec(slip_bf, near_blocks, near_index, far_left, far_right, far_ranks)
    relaxed = slip_rate + jnp.tanh(first_stress / 3.0)
    relaxed_bf = relaxed.astype(jnp.bfloat16)
    second_stress = matvec(relaxed_bf, near_blocks, near_index, far_left, far_right, far_ranks)
    return (first_stress, second_stress)


def solution(mesh):
    in_specs = (
        P(("models", "leaf")),
        P(("models", "leaf"), None, None, None),
        P(("models", "leaf"), None),
        P(None, None, ("models", "leaf")),
        P(None, None, ("models", "leaf")),
        P(("models", "leaf"), None),
    )
    out_specs = (P(("models", "leaf")), P(("models", "leaf")))
    return jax.shard_map(local, mesh=mesh, in_specs=in_specs, out_specs=out_specs, check_vma=False)
```

profile of v0, /device:TPU:38, one launch (start us, length us, event | category | flops | bytes accessed | tf_op | source)
XLA Modules:
  0.0 127.2 jit_solution(1920855411057678525)
XLA Ops:
  0.6 0.0 copy-start.4
  0.6 0.0 copy-start.3
  0.6 0.0 copy-start.5
  0.7 0.9 convert_element_type.20
  1.5 24.0 %collective-permute-start.1 = (bf16[16,256]{1,0:T(8,128)(2,1)S(1)}, bf16[16,256]{1,0:T(8,128)(2,1)S(1)}, u32[]{:S(2)}, u32[]{:S(2)}) collective-permute-start(bf16[16,256]{1,0:T(8,128)(2,1)S(1)} %reshape.104), channel_id=1, source_target_pairs={{1,0},{2,1},{3,2},{4,3},{5,4},{6,5},{7,6},{8,7},{9,8},{10,9},{11,1... | collective-permute-start | bytes 24584 | tf_op jit(solution)/shard_map/ppermute | solution.py:21
  25.5 2.0 %collective-permute-start = (bf16[16,256]{1,0:T(8,128)(2,1)S(1)}, bf16[16,256]{1,0:T(8,128)(2,1)S(1)}, u32[]{:S(2)}, u32[]{:S(2)}) collective-permute-start(bf16[16,256]{1,0:T(8,128)(2,1)S(1)} %reshape.104), channel_id=1, source_target_pairs={{0,1},{1,2},{2,3},{3,4},{4,5},{5,6},{6,7},{7,8},{8,9},{9,10},{10,1... | collective-permute-start | bytes 24584 | tf_op jit(solution)/shard_map/ppermute | solution.py:18
  27.5 3.7 %fusion.6 = f32[16,1,11,32]{3,1,2,0:T(1,128)S(1)} fusion(bf16[16,256,1,1]{1,2,3,0:T(2,128)(2,1)S(1)} %reshape.129, bf16[11,4,16,8,256]{4,3,2,1,0:T(8,128)(2,1)} %bitcast.133), kind=kOutput, calls=%fused_computation.6 | convolution fusion | flops 2883584 | bytes 2914304 | tf_op jit(solution)/shard_map/lrcp,cp->lcr/dot_general | solution.py:53
  31.2 0.1 collective-permute-start.2
  31.4 0.0 copy-done.4
  31.4 0.1 copy.10
  31.5 0.1 iota_compare_fusion.1
  31.9 0.0 copy-done.3
  31.9 0.1 copy.11
  31.9 0.5 collective-permute-done.2
  32.5 0.0 collective-permute-start.3
  32.5 3.6 %collective-permute-done.3 = f32[7,32]{1,0:T(8,128)S(1)} collective-permute-done((f32[7,32]{1,0:T(8,128)S(1)}, f32[7,32]{1,0:T(8,128)S(1)}, u32[]{:S(2)}, u32[]{:S(2)}) %collective-permute-start.3) | collective-permute-done | bytes 928 | tf_op jit(solution)/shard_map/ppermute | solution.py:10
  36.1 0.0 collective-permute-start.4
  36.1 4.5 %collective-permute-done.4 = f32[7,32]{1,0:T(8,128)S(1)} collective-permute-done((f32[7,32]{1,0:T(8,128)S(1)}, f32[7,32]{1,0:T(8,128)S(1)}, u32[]{:S(2)}, u32[]{:S(2)}) %collective-permute-start.4) | collective-permute-done | bytes 928 | tf_op jit(solution)/shard_map/ppermute | solution.py:10
  40.6 0.0 collective-permute-start.5
  40.6 7.5 %collective-permute-done.5 = f32[7,32]{1,0:T(8,128)S(1)} collective-permute-done((f32[7,32]{1,0:T(8,128)S(1)}, f32[7,32]{1,0:T(8,128)S(1)}, u32[]{:S(2)}, u32[]{:S(2)}) %collective-permute-start.5) | collective-permute-done | bytes 928 | tf_op jit(solution)/shard_map/ppermute | solution.py:10
  48.1 1.3 %collective-permute-start.6 = (f32[7,32]{1,0:T(8,128)S(1)}, f32[7,32]{1,0:T(8,128)S(1)}, u32[]{:S(2)}, u32[]{:S(2)}) collective-permute-start(f32[7,32]{1,0:T(8,128)S(1)} %add.49), channel_id=1, source_target_pairs={{0,16},{1,17},{2,18},{3,19},{4,20},{5,21},{6,22},{7,23},{8,24},{9,... | collective-permute-start | bytes 2696 | tf_op jit(solution)/shard_map/ppermute | solution.py:10
  49.5 11.0 %collective-permute-done.6 = f32[7,32]{1,0:T(8,128)S(1)} collective-permute-done((f32[7,32]{1,0:T(8,128)S(1)}, f32[7,32]{1,0:T(8,128)S(1)}, u32[]{:S(2)}, u32[]{:S(2)}) %collective-permute-start.6) | collective-permute-done | bytes 928 | tf_op jit(solution)/shard_map/ppermute | solution.py:10
  60.5 0.4 collective-permute-start.7
  60.9 3.2 %collective-permute-done.7 = f32[7,32]{1,0:T(8,128)S(1)} collective-permute-done((f32[7,32]{1,0:T(8,128)S(1)}, f32[7,32]{1,0:T(8,128)S(1)}, u32[]{:S(2)}, u32[]{:S(2)}) %collective-permute-start.7) | collective-permute-done | bytes 928 | tf_op jit(solution)/shard_map/ppermute | solution.py:10
  64.1 0.8 collective-permute-start.8
  64.9 4.3 %collective-permute-done.8 = f32[7,32]{1,0:T(8,128)S(1)} collective-permute-done((f32[7,32]{1,0:T(8,128)S(1)}, f32[7,32]{1,0:T(8,128)S(1)}, u32[]{:S(2)}, u32[]{:S(2)}) %collective-permute-start.8) | collective-permute-done | bytes 928 | tf_op jit(solution)/shard_map/ppermute | solution.py:10
  69.2 0.1 fusion.18
  69.3 0.0 copy-done.5
  69.3 0.6 fusion.2
  69.9 0.0 collective-permute-done.1
  69.9 0.0 collective-permute-done
  69.9 0.1 convolution_convert_fusion.1
  70.1 0.0 copy-start.1
  70.1 0.0 copy-start
  70.1 4.7 %fusion.16 = f32[16,1,256,1]{2,1,3,0:T(1,128)S(1)} fusion(bf16[16,3,256,256]{3,2,1,0:T(8,128)(2,1)} %param.7, bf16[16,3,256,1]{2,1,0,3:T(4,128)(2,1)S(1)} %bitcast.141), kind=kOutput, calls=%fused_computation.25 | convolution fusion | flops 6291456 | bytes 6332416 | tf_op jit(solution)/shard_map/ikpq,ikq->ip/dot_general | solution.py:51
  74.8 0.0 copy-start.2
  74.8 0.0 copy-done.1
  74.8 2.0 %collective-permute-start.10 = (bf16[16,256]{1,0:T(8,128)(2,1)S(1)}, bf16[16,256]{1,0:T(8,128)(2,1)S(1)}, u32[]{:S(2)}, u32[]{:S(2)}) collective-permute-start(bf16[16,256]{1,0:T(8,128)(2,1)S(1)} %reshape.110), channel_id=1, source_target_pairs={{1,0},{2,1},{3,2},{4,3},{5,4},{6,5},{7,6},{8,7},{9,8},{10,9},{11,1... | collective-permute-start | bytes 24584 | tf_op jit(solution)/shard_map/ppermute | solution.py:21
  76.8 2.4 %collective-permute-start.9 = (bf16[16,256]{1,0:T(8,128)(2,1)S(1)}, bf16[16,256]{1,0:T(8,128)(2,1)S(1)}, u32[]{:S(2)}, u32[]{:S(2)}) collective-permute-start(bf16[16,256]{1,0:T(8,128)(2,1)S(1)} %reshape.110), channel_id=1, source_target_pairs={{0,1},{1,2},{2,3},{3,4},{4,5},{5,6},{6,7},{7,8},{8,9},{9,10},{10,1... | collective-permute-start | bytes 24584 | tf_op jit(solution)/shard_map/ppermute | solution.py:18
  79.2 0.0 copy-done
  79.3 1.9 %fusion.4 = f32[16,1,11,32]{3,1,2,0:T(1,128)S(1)} fusion(bf16[16,256,1,1]{1,2,3,0:T(2,128)(2,1)S(1)} %reshape.131, bf16[11,4,16,8,256]{4,3,2,1,0:T(8,128)(2,1)S(1)} %bitcast.134), kind=kOutput, calls=%fused_computation.4 | convolution fusion | flops 2883584 | bytes 2914304 | tf_op jit(solution)/shard_map/lrcp,cp->lcr/dot_general | solution.py:53
  81.4 0.1 collective-permute-start.11
  81.6 1.1 collective-permute-done.11
  82.7 0.0 collective-permute-start.12
  82.7 3.5 %collective-permute-done.12 = f32[7,32]{1,0:T(8,128)S(1)} collective-permute-done((f32[7,32]{1,0:T(8,128)S(1)}, f32[7,32]{1,0:T(8,128)S(1)}, u32[]{:S(2)}, u32[]{:S(2)}) %collective-permute-start.12) | collective-permute-done | bytes 928 | tf_op jit(solution)/shard_map/ppermute | solution.py:10
  86.3 0.0 collective-permute-start.13
  86.3 4.5 %collective-permute-done.13 = f32[7,32]{1,0:T(8,128)S(1)} collective-permute-done((f32[7,32]{1,0:T(8,128)S(1)}, f32[7,32]{1,0:T(8,128)S(1)}, u32[]{:S(2)}, u32[]{:S(2)}) %collective-permute-start.13) | collective-permute-done | bytes 928 | tf_op jit(solution)/shard_map/ppermute | solution.py:10
  90.8 0.0 collective-permute-start.14
  90.8 7.5 %collective-permute-done.14 = f32[7,32]{1,0:T(8,128)S(1)} collective-permute-done((f32[7,32]{1,0:T(8,128)S(1)}, f32[7,32]{1,0:T(8,128)S(1)}, u32[]{:S(2)}, u32[]{:S(2)}) %collective-permute-start.14) | collective-permute-done | bytes 928 | tf_op jit(solution)/shard_map/ppermute | solution.py:10
  98.3 2.6 %collective-permute-start.15 = (f32[7,32]{1,0:T(8,128)S(1)}, f32[7,32]{1,0:T(8,128)S(1)}, u32[]{:S(2)}, u32[]{:S(2)}) collective-permute-start(f32[7,32]{1,0:T(8,128)S(1)} %add.57), channel_id=1, source_target_pairs={{0,16},{1,17},{2,18},{3,19},{4,20},{5,21},{6,22},{7,23},{8,24},{9,... | collective-permute-start | bytes 2696 | tf_op jit(solution)/shard_map/ppermute | solution.py:10
  100.9 9.7 %collective-permute-done.15 = f32[7,32]{1,0:T(8,128)S(1)} collective-permute-done((f32[7,32]{1,0:T(8,128)S(1)}, f32[7,32]{1,0:T(8,128)S(1)}, u32[]{:S(2)}, u32[]{:S(2)}) %collective-permute-start.15) | collective-permute-done | bytes 928 | tf_op jit(solution)/shard_map/ppermute | solution.py:10
  110.7 0.4 collective-permute-start.16
  111.1 3.2 %collective-permute-done.16 = f32[7,32]{1,0:T(8,128)S(1)} collective-permute-done((f32[7,32]{1,0:T(8,128)S(1)}, f32[7,32]{1,0:T(8,128)S(1)}, u32[]{:S(2)}, u32[]{:S(2)}) %collective-permute-start.16) | collective-permute-done | bytes 928 | tf_op jit(solution)/shard_map/ppermute | solution.py:10
  114.3 0.8 collective-permute-start.17
  115.1 4.3 %collective-permute-done.17 = f32[7,32]{1,0:T(8,128)S(1)} collective-permute-done((f32[7,32]{1,0:T(8,128)S(1)}, f32[7,32]{1,0:T(8,128)S(1)}, u32[]{:S(2)}, u32[]{:S(2)}) %collective-permute-start.17) | collective-permute-done | bytes 928 | tf_op jit(solution)/shard_map/ppermute | solution.py:10
  119.4 0.1 fusion.19
  119.5 2.4 %fusion = f32[16,1,256,1]{2,1,3,0:T(1,128)S(1)} fusion(bf16[11,4,16,8,256]{4,3,2,1,0:T(8,128)(2,1)} %bitcast.167, bf16[11,16,32,1]{2,1,0,3:T(8,128)(2,1)S(1)} %fusion.19), kind=kOutput, calls=%fused_computation | convolution fusion | flops 2883584 | bytes 2911232 | tf_op jit(solution)/shard_map/lrcp,lcr->cp/dot_general | solution.py:80
  121.9 0.0 copy-done.2
  121.9 0.0 collective-permute-done.10
  121.9 0.0 collective-permute-done.9
  121.9 0.1 convolution_convert_fusion
  122.0 4.5 %fusion.14 = f32[16,1,256,1]{2,1,3,0:T(1,128)S(1)} fusion(bf16[16,3,256,256]{3,2,1,0:T(8,128)(2,1)} %param.7, bf16[16,3,256,1]{2,1,0,3:T(4,128)(2,1)S(1)} %bitcast.142), kind=kOutput, calls=%fused_computation.23 | convolution fusion | flops 6291456 | bytes 6332416 | tf_op jit(solution)/shard_map/ikpq,ikq->ip/dot_general | solution.py:51
  126.5 0.6 copy.36
  (91 shorter events, 1.0 us)
Async XLA Ops:
  0.6 30.8 %copy-start.4 = (s32[16,3]{0,1:T(4,128)S(1)}, s32[16,3]{0,1:T(4,128)}, u32[]{:S(2)}) copy-start(s32[16,3]{0,1:T(4,128)} %param.8) | copy-start | bytes 580
  0.6 31.2 %copy-start.3 = (s32[16,11]{1,0:T(8,128)S(1)}, s32[16,11]{1,0:T(8,128)}, u32[]{:S(2)}) copy-start(s32[16,11]{1,0:T(8,128)} %param.11) | copy-start | bytes 2116
  0.6 68.7 %copy-start.5 = (bf16[11,32,4096]{2,1,0:T(8,128)(2,1)S(1)}, bf16[11,32,4096]{2,1,0:T(8,128)(2,1)}, u32[]{:S(2)}) copy-start(bf16[11,32,4096]{2,1,0:T(8,128)(2,1)} %param.9) | copy-start | bytes 8650756
  1.5 68.3 %collective-permute-start.1 = (bf16[16,256]{1,0:T(8,128)(2,1)S(1)}, bf16[16,256]{1,0:T(8,128)(2,1)S(1)}, u32[]{:S(2)}, u32[]{:S(2)}) collective-permute-start(bf16[16,256]{1,0:T(8,128)(2,1)S(1)} %reshape.104), channel_id=1, source_target_pairs={{1,0},{2,1},{3,2},{4,3},{5,4},{6,5},{7,6},{8,7},{9,8},{10,9},{11,1... | collective-permute-start | bytes 24584 | tf_op jit(solution)/shard_map/ppermute | solution.py:21
  25.5 44.4 %collective-permute-start = (bf16[16,256]{1,0:T(8,128)(2,1)S(1)}, bf16[16,256]{1,0:T(8,128)(2,1)S(1)}, u32[]{:S(2)}, u32[]{:S(2)}) collective-permute-start(bf16[16,256]{1,0:T(8,128)(2,1)S(1)} %reshape.104), channel_id=1, source_target_pairs={{0,1},{1,2},{2,3},{3,4},{4,5},{5,6},{6,7},{7,8},{8,9},{9,10},{10,1... | collective-permute-start | bytes 24584 | tf_op jit(solution)/shard_map/ppermute | solution.py:18
  31.2 1.3 %collective-permute-start.2 = (f32[7,32]{1,0:T(8,128)S(1)}, f32[7,32]{1,0:T(8,128)S(1)}, u32[]{:S(2)}, u32[]{:S(2)}) collective-permute-start(f32[7,32]{1,0:T(8,128)S(1)} %slice_reduce_fusion.1), channel_id=1, source_target_pairs={{0,1},{1,0},{2,3},{3,2},{4,5},{5,4},{6,7},{7,6},{8,9},{9,8},{10,11... | collective-permute-start | bytes 2696 | tf_op jit(solution)/shard_map/ppermute | solution.py:10
  32.5 3.6 %collective-permute-start.3 = (f32[7,32]{1,0:T(8,128)S(1)}, f32[7,32]{1,0:T(8,128)S(1)}, u32[]{:S(2)}, u32[]{:S(2)}) collective-permute-start(f32[7,32]{1,0:T(8,128)S(1)} %add.46), channel_id=1, source_target_pairs={{0,2},{1,3},{2,0},{3,1},{4,6},{5,7},{6,4},{7,5},{8,10},{9,11},{10,... | collective-permute-start | bytes 2696 | tf_op jit(solution)/shard_map/ppermute | solution.py:10
  36.1 4.5 %collective-permute-start.4 = (f32[7,32]{1,0:T(8,128)S(1)}, f32[7,32]{1,0:T(8,128)S(1)}, u32[]{:S(2)}, u32[]{:S(2)}) collective-permute-start(f32[7,32]{1,0:T(8,128)S(1)} %add.47), channel_id=1, source_target_pairs={{0,4},{1,5},{2,6},{3,7},{4,0},{5,1},{6,2},{7,3},{8,12},{9,13},{10,... | collective-permute-start | bytes 2696 | tf_op jit(solution)/shard_map/ppermute | solution.py:10
  40.6 7.5 %collective-permute-start.5 = (f32[7,32]{1,0:T(8,128)S(1)}, f32[7,32]{1,0:T(8,128)S(1)}, u32[]{:S(2)}, u32[]{:S(2)}) collective-permute-start(f32[7,32]{1,0:T(8,128)S(1)} %add.48), channel_id=1, source_target_pairs={{0,8},{1,9},{2,10},{3,11},{4,12},{5,13},{6,14},{7,15},{8,0},{9,1},... | collective-permute-start | bytes 2696 | tf_op jit(solution)/shard_map/ppermute | solution.py:10
  48.1 12.3 %collective-permute-start.6 = (f32[7,32]{1,0:T(8,128)S(1)}, f32[7,32]{1,0:T(8,128)S(1)}, u32[]{:S(2)}, u32[]{:S(2)}) collective-permute-start(f32[7,32]{1,0:T(8,128)S(1)} %add.49), channel_id=1, source_target_pairs={{0,16},{1,17},{2,18},{3,19},{4,20},{5,21},{6,22},{7,23},{8,24},{9,... | collective-permute-start | bytes 2696 | tf_op jit(solution)/shard_map/ppermute | solution.py:10
  60.5 3.6 %collective-permute-start.7 = (f32[7,32]{1,0:T(8,128)S(1)}, f32[7,32]{1,0:T(8,128)S(1)}, u32[]{:S(2)}, u32[]{:S(2)}) collective-permute-start(f32[7,32]{1,0:T(8,128)S(1)} %add.50), channel_id=1, source_target_pairs={{0,32},{1,33},{2,34},{3,35},{4,36},{5,37},{6,38},{7,39},{8,40},{9,... | collective-permute-start | bytes 2696 | tf_op jit(solution)/shard_map/ppermute | solution.py:10
  64.1 5.1 %collective-permute-start.8 = (f32[7,32]{1,0:T(8,128)S(1)}, f32[7,32]{1,0:T(8,128)S(1)}, u32[]{:S(2)}, u32[]{:S(2)}) collective-permute-start(f32[7,32]{1,0:T(8,128)S(1)} %add.51), channel_id=1, source_target_pairs={{0,64},{1,65},{2,66},{3,67},{4,68},{5,69},{6,70},{7,71},{8,72},{9,... | collective-permute-start | bytes 2696 | tf_op jit(solution)/shard_map/ppermute | solution.py:10
  70.1 4.7 %copy-start.1 = (f32[4096]{0:T(1024)S(1)}, f32[4096]{0:T(1024)}, u32[]{:S(2)}) copy-start(f32[4096]{0:T(1024)} %param.6) | copy-start | bytes 49156
  70.1 9.2 %copy-start = (bf16[11,32,4096]{2,1,0:T(8,128)(2,1)S(1)}, bf16[11,32,4096]{2,1,0:T(8,128)(2,1)}, u32[]{:S(2)}) copy-start(bf16[11,32,4096]{2,1,0:T(8,128)(2,1)} %param.10) | copy-start | bytes 8650756
  74.8 47.1 %copy-start.2 = (f32[2,2,8,128]{3,1,2,0:T(2,128)}, f32[2,2,8,128]{3,1,2,0:T(2,128)S(1)}, u32[]{:S(2)}) copy-start(f32[2,2,8,128]{3,1,2,0:T(2,128)S(1)} %copy.35) | copy-start | bytes 49156
  74.8 47.0 %collective-permute-start.10 = (bf16[16,256]{1,0:T(8,128)(2,1)S(1)}, bf16[16,256]{1,0:T(8,128)(2,1)S(1)}, u32[]{:S(2)}, u32[]{:S(2)}) collective-permute-start(bf16[16,256]{1,0:T(8,128)(2,1)S(1)} %reshape.110), channel_id=1, source_target_pairs={{1,0},{2,1},{3,2},{4,3},{5,4},{6,5},{7,6},{8,7},{9,8},{10,9},{11,1... | collective-permute-start | bytes 24584 | tf_op jit(solution)/shard_map/ppermute | solution.py:21
  76.8 45.1 %collective-permute-start.9 = (bf16[16,256]{1,0:T(8,128)(2,1)S(1)}, bf16[16,256]{1,0:T(8,128)(2,1)S(1)}, u32[]{:S(2)}, u32[]{:S(2)}) collective-permute-start(bf16[16,256]{1,0:T(8,128)(2,1)S(1)} %reshape.110), channel_id=1, source_target_pairs={{0,1},{1,2},{2,3},{3,4},{4,5},{5,6},{6,7},{7,8},{8,9},{9,10},{10,1... | collective-permute-start | bytes 24584 | tf_op jit(solution)/shard_map/ppermute | solution.py:18
  81.4 1.3 %collective-permute-start.11 = (f32[7,32]{1,0:T(8,128)S(1)}, f32[7,32]{1,0:T(8,128)S(1)}, u32[]{:S(2)}, u32[]{:S(2)}) collective-permute-start(f32[7,32]{1,0:T(8,128)S(1)} %slice_reduce_fusion), channel_id=1, source_target_pairs={{0,1},{1,0},{2,3},{3,2},{4,5},{5,4},{6,7},{7,6},{8,9},{9,8},{10,11... | collective-permute-start | bytes 2696 | tf_op jit(solution)/shard_map/ppermute | solution.py:10
  82.7 3.6 %collective-permute-start.12 = (f32[7,32]{1,0:T(8,128)S(1)}, f32[7,32]{1,0:T(8,128)S(1)}, u32[]{:S(2)}, u32[]{:S(2)}) collective-permute-start(f32[7,32]{1,0:T(8,128)S(1)} %add.54), channel_id=1, source_target_pairs={{0,2},{1,3},{2,0},{3,1},{4,6},{5,7},{6,4},{7,5},{8,10},{9,11},{10,... | collective-permute-start | bytes 2696 | tf_op jit(solution)/shard_map/ppermute | solution.py:10
  86.3 4.5 %collective-permute-start.13 = (f32[7,32]{1,0:T(8,128)S(1)}, f32[7,32]{1,0:T(8,128)S(1)}, u32[]{:S(2)}, u32[]{:S(2)}) collective-permute-start(f32[7,32]{1,0:T(8,128)S(1)} %add.55), channel_id=1, source_target_pairs={{0,4},{1,5},{2,6},{3,7},{4,0},{5,1},{6,2},{7,3},{8,12},{9,13},{10,... | collective-permute-start | bytes 2696 | tf_op jit(solution)/shard_map/ppermute | solution.py:10
  90.8 7.5 %collective-permute-start.14 = (f32[7,32]{1,0:T(8,128)S(1)}, f32[7,32]{1,0:T(8,128)S(1)}, u32[]{:S(2)}, u32[]{:S(2)}) collective-permute-start(f32[7,32]{1,0:T(8,128)S(1)} %add.56), channel_id=1, source_target_pairs={{0,8},{1,9},{2,10},{3,11},{4,12},{5,13},{6,14},{7,15},{8,0},{9,1},... | collective-permute-start | bytes 2696 | tf_op jit(solution)/shard_map/ppermute | solution.py:10
  98.3 12.3 %collective-permute-start.15 = (f32[7,32]{1,0:T(8,128)S(1)}, f32[7,32]{1,0:T(8,128)S(1)}, u32[]{:S(2)}, u32[]{:S(2)}) collective-permute-start(f32[7,32]{1,0:T(8,128)S(1)} %add.57), channel_id=1, source_target_pairs={{0,16},{1,17},{2,18},{3,19},{4,20},{5,21},{6,22},{7,23},{8,24},{9,... | collective-permute-start | bytes 2696 | tf_op jit(solution)/shard_map/ppermute | solution.py:10
  110.7 3.6 %collective-permute-start.16 = (f32[7,32]{1,0:T(8,128)S(1)}, f32[7,32]{1,0:T(8,128)S(1)}, u32[]{:S(2)}, u32[]{:S(2)}) collective-permute-start(f32[7,32]{1,0:T(8,128)S(1)} %add.58), channel_id=1, source_target_pairs={{0,32},{1,33},{2,34},{3,35},{4,36},{5,37},{6,38},{7,39},{8,40},{9,... | collective-permute-start | bytes 2696 | tf_op jit(solution)/shard_map/ppermute | solution.py:10
  114.3 5.1 %collective-permute-start.17 = (f32[7,32]{1,0:T(8,128)S(1)}, f32[7,32]{1,0:T(8,128)S(1)}, u32[]{:S(2)}, u32[]{:S(2)}) collective-permute-start(f32[7,32]{1,0:T(8,128)S(1)} %add.59), channel_id=1, source_target_pairs={{0,64},{1,65},{2,66},{3,67},{4,68},{5,69},{6,70},{7,71},{8,72},{9,... | collective-permute-start | bytes 2696 | tf_op jit(solution)/shard_map/ppermute | solution.py:10
where the time goes:
time: 127 us
  waiting for transfers between devices  68.3 us (54%)
  starting transfers between devices  37 us (29%)
  matrix products  17.9 us (14%)
  other arithmetic  1.49 us (1%)
  local copies, waits for them, and re-layouts  1.47 us (1%)
    ppermute x14, waiting for transfers between devices, partner_2(): lax.ppermute(value, axis, [(i, i ^ 1 << stride) for i in range(lax.axis_s...  68.3 us
    ppermute x2, starting transfers between devices, padded(): lax.ppermute(lax.slice_in_dim(block, 0, width, axis=dim), axis, backward)  25.9 us
    dot_general x2, matrix products, matvec(): jnp.einsum('ikpq,ikq->ip', near_blocks, picked, preferred_element_type=jn...  9.15 us
    ppermute x14, starting transfers between devices, partner_2(): lax.ppermute(value, axis, [(i, i ^ 1 << stride) for i in range(lax.axis_s...  6.72 us
    dot_general x2, matrix products, matvec(): jnp.einsum('lrcp,cp->lcr', right_part, slip_rows, preferred_element_type=...  5.54 us
    ppermute x2, starting transfers between devices, padded(): lax.ppermute(lax.slice_in_dim(block, block.shape[dim] - width, None, axis...  4.39 us
    dot_general x2, matrix products, matvec(): jnp.einsum('lrcp,lcr->cp', left_part, weights, preferred_element_type=jnp...  2.95 us
  transfers between devices with their start and end apart: 18, of which 14 were waited for; matrix products, arithmetic and copies ran while one was open for 8% of the time, Pallas kernels for 0%

commit v1 on v0

v1 whole, which is shorter than its diff:
```python
import functools
import math

import jax
import jax.numpy as jnp
from jax import lax
from jax.experimental import pallas as pl
from jax.experimental.pallas import tpu as pltpu
from jax.sharding import PartitionSpec as P

MESH = pl.DeviceIdType.MESH
F32 = jnp.float32
BF16 = jnp.bfloat16
LANES = 128
FAR_BITS = 2
NT = (((1,), (1,)), ((), ()))
NN = (((1,), (0,)), ((), ()))


def dot(a, b, dims):
    return lax.dot_general(a, b, dims, preferred_element_type=F32)


def kernel(
    shape,
    slip_hbm, ranks_hbm, index_hbm, right_hbm, near_hbm, left_hbm,
    first_hbm, second_hbm,
    slip, ranks, index, right, near, left, out, own, halo, masks,
    sums, got, plane_sums, got_far,
    load_sem, out_sem, halo_send, halo_recv, sums_send, sums_recv, far_send, far_recv,
):
    count, leaves, nears, leaf, levels, rank = shape
    local_levels = leaves.bit_length() - 1
    cross = levels - local_levels
    plane_bits = cross - FAR_BITS
    plane = 2**plane_bits
    groups = 2**FAR_BITS
    me = lax.axis_index("leaf")

    def peer_of(delta):
        return jnp.bitwise_xor(me, delta)

    right_of = lax.rem(me + 1, count)
    left_of = lax.rem(me + count - 1, count)

    barrier = pltpu.get_barrier_semaphore()
    peers = [right_of, left_of]
    peers += [peer_of(t) for t in range(1, plane)]
    peers += [peer_of(plane * g) for g in range(1, groups)]
    for peer in peers:
        pl.semaphore_signal(barrier, inc=1, device_id={"leaf": peer}, device_id_type=MESH)

    high = local_levels - 1
    loads = [
        pltpu.make_async_copy(slip_hbm, slip, load_sem.at[0]),
        pltpu.make_async_copy(right_hbm.at[pl.ds(high, levels - high)],
                              right.at[pl.ds(high, levels - high)], load_sem.at[1]),
        pltpu.make_async_copy(ranks_hbm, ranks, load_sem.at[2]),
        pltpu.make_async_copy(index_hbm, index, load_sem.at[3]),
        pltpu.make_async_copy(right_hbm.at[pl.ds(0, high)], right.at[pl.ds(0, high)], load_sem.at[4]),
        pltpu.make_async_copy(near_hbm, near, load_sem.at[5]),
        pltpu.make_async_copy(left_hbm, left, load_sem.at[6]),
    ]
    for load in loads:
        load.start()

    row = lax.broadcasted_iota(jnp.int32, (leaves, leaf), 0)
    row_l = lax.broadcasted_iota(jnp.int32, (leaves, LANES), 0)
    lane = lax.broadcasted_iota(jnp.int32, (leaves, LANES), 1)
    lane1 = lax.broadcasted_iota(jnp.int32, (1, LANES), 1)

    def project(vf, start, stop):
        rows = (stop - start) * rank
        total = jnp.zeros((leaves, rows), F32)
        for c in range(leaves):
            lhs = jnp.where(row == c, vf, 0.0).astype(BF16)
            rhs = right[start:stop, :, c * leaf:(c + 1) * leaf].reshape(rows, leaf)
            total += dot(lhs, rhs, NT)
        return total

    def apply_far(total, weights, start, stop):
        rows = (stop - start) * rank
        row_w = lax.broadcasted_iota(jnp.int32, weights.shape, 0)
        for i in range(leaves):
            lhs = jnp.where(row_w == i, weights, 0.0).astype(BF16)[:, :rows]
            rhs = left[start:stop, :, i * leaf:(i + 1) * leaf].reshape(rows, leaf)
            total += dot(lhs, rhs, NN)
        return total

    def scale_of(level):
        return 1.0 / math.sqrt(leaf * 2**level)

    def product(step, vf):
        own[step] = vf.astype(BF16)
        if step == 0:
            loads[1].wait()
        summed = project(vf, high, levels)
        device_sums = jnp.sum(summed, axis=0, keepdims=True)
        parts = [device_sums[:, :LANES], device_sums[:, LANES:]]
        for b in range(plane_bits):
            place = (b + 1) * rank
            shift = (rank - place) % LANES
            source = parts[place // LANES]
            moved = pltpu.roll(source, shift, 1) if shift else source
            sums[step, b] = jnp.where(lane1 < 2 * rank, moved, parts[1])
        if step == 0:
            pl.semaphore_wait(barrier, len(peers))
        for t in range(1, plane):
            pltpu.make_async_remote_copy(
                src_ref=sums.at[step, t.bit_length() - 1],
                dst_ref=got.at[step, t],
                send_sem=sums_send.at[step],
                recv_sem=sums_recv.at[step],
                device_id={"leaf": peer_of(t)},
                device_id_type=MESH,
            ).start()
        halos = []
        for side, peer in ((0, right_of), (1, left_of)):
            copy = pltpu.make_async_remote_copy(
                src_ref=own.at[step],
                dst_ref=halo.at[step, side],
                send_sem=halo_send.at[step, side],
                recv_sem=halo_recv.at[step, side],
                device_id={"leaf": peer},
                device_id_type=MESH,
            )
            copy.start()
            halos.append(copy)

        if step == 0:
            loads[2].wait()
            loads[3].wait()
            for group in range(-(-levels * rank // LANES)):
                limit = jnp.zeros((leaves, LANES), jnp.int32)
                for part in range(LANES // rank):
                    level = group * (LANES // rank) + part
                    if level < levels:
                        held = jnp.broadcast_to(ranks[:, level:level + 1], (leaves, LANES))
                        limit = jnp.where(lane // rank == part, held, limit)
                masks[group] = (lane % rank < limit).astype(F32)
            loads[4].wait()

        below = project(vf, 0, high)
        chosen = jnp.zeros((leaves, LANES), F32)
        fine = jnp.concatenate([below, summed[:, :rank]], axis=1)
        cluster_r = lax.broadcasted_iota(jnp.int32, (leaves, leaves), 0)
        cluster_c = lax.broadcasted_iota(jnp.int32, (leaves, leaves), 1)
        for level in range(local_levels):
            pick = (cluster_c >> level) == ((cluster_r >> level) ^ 1)
            partner = lax.dot_general(
                pick.astype(F32), fine, NN,
                precision=lax.Precision.HIGHEST, preferred_element_type=F32,
            )
            chosen = jnp.where(lane // rank == level, partner * scale_of(level), chosen)
        if step == 0:
            loads[6].wait()
        total = apply_far(
            jnp.zeros((leaves, leaf), F32), jnp.where(masks[0] > 0.0, chosen, 0.0), 0, local_levels
        )

        for copy in halos:
            copy.wait_recv()
        if step == 0:
            loads[5].wait()
        extended = jnp.concatenate([halo[step, 0], own[step], halo[step, 1]], axis=0)
        first_leaf = (me - 1) * leaves
        spot = lax.broadcasted_iota(jnp.int32, (leaves, 3 * leaves), 1) + first_leaf
        for k in range(nears):
            hot = (jnp.broadcast_to(index[:, k:k + 1], (leaves, 3 * leaves)) == spot)
            picked = dot(hot.astype(F32).astype(BF16), extended, NN)
            for i in range(leaves):
                lhs = jnp.where(row == i, picked, 0.0).astype(BF16)
                total += dot(lhs, near[i, k], NT)

        pltpu.make_async_copy(
            got.at[step, pl.ds(1, plane - 1)], got.at[step, pl.ds(1, plane - 1)], sums_recv.at[step]
        ).wait()
        by_level = []
        for b in range(plane_bits):
            terms = [got[step, t] for t in range(2**b, 2 ** (b + 1))]
            while len(terms) > 1:
                terms = [x + y for x, y in zip(terms[::2], terms[1::2])]
            by_level.append(terms[0])
        everything = parts[1]
        for term in by_level:
            everything = everything + term
        plane_sums[step] = everything
        for g in range(1, groups):
            pltpu.make_async_remote_copy(
                src_ref=plane_sums.at[step],
                dst_ref=got_far.at[step, g],
                send_sem=far_send.at[step],
                recv_sem=far_recv.at[step],
                device_id={"leaf": peer_of(plane * g)},
                device_id_type=MESH,
            ).start()
        per = LANES // rank
        columns = []
        for group in range(-(-plane_bits // per)):
            held = jnp.zeros((1, LANES), F32)
            for part in range(per):
                b = group * per + part
                if b < plane_bits:
                    shift = (part - 1) * rank % LANES
                    value = by_level[b] * scale_of(local_levels + b)
                    value = pltpu.roll(value, shift, 1) if shift else value
                    held = jnp.where(lane1 // rank == part, value, held)
            columns.append(
                jnp.where(masks[group + 1] > 0.0, jnp.broadcast_to(held, (leaves, LANES)), 0.0)
            )
        total = apply_far(
            total, jnp.concatenate(columns, axis=1), local_levels, local_levels + plane_bits
        )

        pltpu.make_async_copy(
            got_far.at[step, pl.ds(1, groups - 1)], got_far.at[step, pl.ds(1, groups - 1)],
            far_recv.at[step],
        ).wait()
        near_far = got_far[step, 1] * scale_of(levels - 2)
        far_far = (got_far[step, 2] + got_far[step, 3]) * scale_of(levels - 1)
        held = jnp.where(lane1 < 3 * rank, near_far, far_far)
        held = pltpu.roll(held, 2 * rank, 1)
        shift = (plane_bits + local_levels) * rank % LANES
        mask = pltpu.roll(masks[(plane_bits + local_levels) * rank // LANES], (LANES - shift) % LANES, 1)
        last = jnp.where(mask > 0.0, jnp.broadcast_to(held, (leaves, LANES)), 0.0)
        total = apply_far(total, last, levels - FAR_BITS, levels)
        out[step, pl.ds(0, leaves, 2), :] = total[:, :LANES]
        out[step, pl.ds(1, leaves, 2), :] = total[:, LANES:]
        return total

    loads[0].wait()
    slip_rate = jnp.concatenate([slip[pl.ds(0, leaves, 2), :], slip[pl.ds(1, leaves, 2), :]], axis=1)
    first = product(0, slip_rate.astype(BF16).astype(F32))
    first_out = pltpu.make_async_copy(out.at[0], first_hbm, out_sem.at[0])
    first_out.start()
    relaxed = slip_rate + jnp.tanh(first / 3.0)
    product(1, relaxed.astype(BF16).astype(F32))
    second_out = pltpu.make_async_copy(out.at[1], second_hbm, out_sem.at[1])
    second_out.start()

    for step in range(2):
        for side in range(2):
            pltpu.make_async_copy(own.at[step], own.at[step], halo_send.at[step, side]).wait()
        pltpu.make_async_copy(
            got.at[step, pl.ds(1, plane - 1)], got.at[step, pl.ds(1, plane - 1)], sums_send.at[step]
        ).wait()
        pltpu.make_async_copy(
            got_far.at[step, pl.ds(1, groups - 1)], got_far.at[step, pl.ds(1, groups - 1)],
            far_send.at[step],
        ).wait()
    first_out.wait()
    second_out.wait()


def local(count, slip_rate, near_blocks, near_index, far_left, far_right, far_ranks):
    leaves, nears, leaf, _ = near_blocks.shape
    levels, rank, patches = far_left.shape
    cross = levels - (leaves.bit_length() - 1)
    plane_bits = cross - FAR_BITS
    plane, groups = 2**plane_bits, 2**FAR_BITS
    assert leaf == 2 * LANES and 4 * rank == LANES and 2**cross == count
    flat = (patches // LANES, LANES)
    anywhere = pl.BlockSpec(memory_space=pl.ANY)
    first, second = pl.pallas_call(
        functools.partial(kernel, (count, leaves, nears, leaf, levels, rank)),
        out_shape=[jax.ShapeDtypeStruct(flat, F32)] * 2,
        in_specs=[anywhere] * 6,
        out_specs=[anywhere] * 2,
        scratch_shapes=[
            pltpu.VMEM(flat, F32),
            pltpu.VMEM(far_ranks.shape, jnp.int32),
            pltpu.VMEM(near_index.shape, jnp.int32),
            pltpu.VMEM(far_right.shape, BF16),
            pltpu.VMEM(near_blocks.shape, BF16),
            pltpu.VMEM(far_left.shape, BF16),
            pltpu.VMEM((2,) + flat, F32),
            pltpu.VMEM((2, leaves, leaf), BF16),
            pltpu.VMEM((2, 2, leaves, leaf), BF16),
            pltpu.VMEM((-(-levels * rank // LANES), leaves, LANES), F32),
            pltpu.VMEM((2, plane_bits, 1, LANES), F32),
            pltpu.VMEM((2, plane, 1, LANES), F32),
            pltpu.VMEM((2, 1, LANES), F32),
            pltpu.VMEM((2, groups, 1, LANES), F32),
            pltpu.SemaphoreType.DMA((7,)),
            pltpu.SemaphoreType.DMA((2,)),
            pltpu.SemaphoreType.DMA((2, 2)),
            pltpu.SemaphoreType.DMA((2, 2)),
            pltpu.SemaphoreType.DMA((2,)),
            pltpu.SemaphoreType.DMA((2,)),
            pltpu.SemaphoreType.DMA((2,)),
            pltpu.SemaphoreType.DMA((2,)),
        ],
        compiler_params=pltpu.CompilerParams(collective_id=0, has_side_effects=True),
        name="hmatrix",
    )(slip_rate.reshape(flat), far_ranks, near_index, far_right, near_blocks, far_left)
    return first.reshape(-1), second.reshape(-1)


def solution(mesh):
    both = ("models", "leaf")
    in_specs = (
        P(both), P(both, None, None, None), P(both, None),
        P(None, None, both), P(None, None, both), P(both, None),
    )
    return jax.shard_map(
        functools.partial(local, mesh.shape["leaf"]), mesh=mesh, in_specs=in_specs,
        out_specs=(P(both), P(both)), check_vma=False,
    )
```

time: 127 us -> 55.3 us (0.44)
  the two profiles are of different devices: /device:TPU:38 before, /device:TPU:33 now
where the time goes in v1:
time: 55.3 us; the launch traced here: 54.8 us
  Pallas kernels  50.2 us (91%)
  local copies, waits for them, and re-layouts  4 us (7%)
  between operations  0.64 us (1%)
    pallas_call x1, Pallas kernels, local(): pl.pallas_call(functools.partial(kernel, (count, leaves, nears, leaf, lev...  50.2 us
    unnamed x3, local copies, waits for them, and re-layouts  4 us

profile of v1, /device:TPU:33, one launch (start us, length us, event | category | flops | bytes accessed | tf_op | source)
XLA Modules:
  0.0 54.8 jit_solution(12959517698354868512)
XLA Ops:
  0.6 1.4 %copy.8.index_hbm = s32[16,3]{1,0:T(8,128)} copy(s32[16,3]{0,1:T(4,128)} %param.8) | data formatting | bytes 384 | tf_op args[2]
  2.0 50.2 %hmatrix.1 = (f32[32,128]{1,0:T(8,128)}, f32[32,128]{1,0:T(8,128)}) custom-call(f32[32,128]{1,0:T(8,128)} %bitcast.3, s32[16,11]{1,0:T(8,128)} %ranks_hbm.1, s32[16,3]{1,0:T(8,128)} %copy.8.index_hbm, bf16[11,32,4096]{2,1,0:T(8,128)(2,1)} %right_hbm.1, bf16[16,3,256,256]{3,2,1,0:T(8,128)(2,1)} %near_hbm.1, bf16[11,32,4096]{2,1,0:T(8,128)(2,1)} %left_hbm.1), custom_call_target="tpu_custom_call" | custom-call | tf_op jit(solution)/shard_map/hmatrix/pallas_call | solution.py:264
  52.2 1.3 %copy.11 = f32[4096]{0:T(1024)} copy(f32[4096]{0:T(1024)} %bitcast.5) | data formatting | bytes 32768
  53.5 1.3 %copy.12 = f32[4096]{0:T(1024)} copy(f32[4096]{0:T(1024)} %bitcast.4) | data formatting | bytes 32768

commit v2 on v1

--- a/solution.py
+++ b/solution.py
@@ -15,6 +15,8 @@
 FAR_BITS = 2
 NT = (((1,), (1,)), ((), ()))
 NN = (((1,), (0,)), ((), ()))
+TN = (((0,), (0,)), ((), ()))
+PIECES = 4
 
 
 def dot(a, b, dims):
@@ -24,10 +26,10 @@
 def kernel(
     shape,
     slip_hbm, ranks_hbm, index_hbm, right_hbm, near_hbm, left_hbm,
-    first_hbm, second_hbm,
-    slip, ranks, index, right, near, left, out, own, halo, masks,
+    out,
+    slip, ranks, index, right, near, left, own, halo, masks,
     sums, got, plane_sums, got_far,
-    load_sem, out_sem, halo_send, halo_recv, sums_send, sums_recv, far_send, far_recv,
+    load_sem, piece_sem, halo_send, halo_recv, sums_send, sums_recv, far_send, far_recv,
 ):
     count, leaves, nears, leaf, levels, rank = shape
     local_levels = leaves.bit_length() - 1
@@ -43,25 +45,36 @@
     right_of = lax.rem(me + 1, count)
     left_of = lax.rem(me + count - 1, count)
 
-    barrier = pltpu.get_barrier_semaphore()
-    peers = [right_of, left_of]
-    peers += [peer_of(t) for t in range(1, plane)]
-    peers += [peer_of(plane * g) for g in range(1, groups)]
-    for peer in peers:
-        pl.semaphore_signal(barrier, inc=1, device_id={"leaf": peer}, device_id_type=MESH)
+    chips = plane // 2
+    def reach(t):
+        return max(min(abs(z - (z ^ t // 2)), chips - abs(z - (z ^ t // 2))) for z in range(chips))
+    deltas = sorted(range(1, plane), key=reach, reverse=True)
 
     high = local_levels - 1
+    piece = leaves // PIECES * leaf
     loads = [
         pltpu.make_async_copy(slip_hbm, slip, load_sem.at[0]),
-        pltpu.make_async_copy(right_hbm.at[pl.ds(high, levels - high)],
-                              right.at[pl.ds(high, levels - high)], load_sem.at[1]),
+        pltpu.make_async_copy(left_hbm, left, load_sem.at[1]),
         pltpu.make_async_copy(ranks_hbm, ranks, load_sem.at[2]),
         pltpu.make_async_copy(index_hbm, index, load_sem.at[3]),
         pltpu.make_async_copy(right_hbm.at[pl.ds(0, high)], right.at[pl.ds(0, high)], load_sem.at[4]),
         pltpu.make_async_copy(near_hbm, near, load_sem.at[5]),
-        pltpu.make_async_copy(left_hbm, left, load_sem.at[6]),
     ]
-    for load in loads:
+    pieces = []
+    for n in range(PIECES):
+        part = (pl.ds(high, levels - high), slice(None), pl.ds(n * piece, piece))
+        pieces.append(pltpu.make_async_copy(right_hbm.at[part], right.at[part], piece_sem.at[n]))
+    loads[0].start()
+    for load in pieces:
+        load.start()
+
+    barrier = pltpu.get_barrier_semaphore()
+    peers = [peer_of(t) for t in deltas]
+    peers += [peer_of(plane * g) for g in range(1, groups)]
+    peers += [right_of, left_of]
+    for peer in peers:
+        pl.semaphore_signal(barrier, inc=1, device_id={"leaf": peer}, device_id_type=MESH)
+    for load in (loads[2], loads[3], loads[4], loads[1], loads[5]):
         load.start()
 
     row = lax.broadcasted_iota(jnp.int32, (leaves, leaf), 0)
@@ -69,10 +82,12 @@
     lane = lax.broadcasted_iota(jnp.int32, (leaves, LANES), 1)
     lane1 = lax.broadcasted_iota(jnp.int32, (1, LANES), 1)
 
-    def project(vf, start, stop):
+    def project(vf, start, stop, ready=()):
         rows = (stop - start) * rank
         total = jnp.zeros((leaves, rows), F32)
         for c in range(leaves):
+            if ready and c % (leaves // PIECES) == 0:
+                ready[c // (leaves // PIECES)].wait()
             lhs = jnp.where(row == c, vf, 0.0).astype(BF16)
             rhs = right[start:stop, :, c * leaf:(c + 1) * leaf].reshape(rows, leaf)
             total += dot(lhs, rhs, NT)
@@ -92,9 +107,7 @@
 
     def product(step, vf):
         own[step] = vf.astype(BF16)
-        if step == 0:
-            loads[1].wait()
-        summed = project(vf, high, levels)
+        summed = project(vf, high, levels, () if step else pieces)
         device_sums = jnp.sum(summed, axis=0, keepdims=True)
         parts = [device_sums[:, :LANES], device_sums[:, LANES:]]
         for b in range(plane_bits):
@@ -105,7 +118,7 @@
             sums[step, b] = jnp.where(lane1 < 2 * rank, moved, parts[1])
         if step == 0:
             pl.semaphore_wait(barrier, len(peers))
-        for t in range(1, plane):
+        for t in deltas:
             pltpu.make_async_remote_copy(
                 src_ref=sums.at[step, t.bit_length() - 1],
                 dst_ref=got.at[step, t],
@@ -153,7 +166,7 @@
             )
             chosen = jnp.where(lane // rank == level, partner * scale_of(level), chosen)
         if step == 0:
-            loads[6].wait()
+            loads[1].wait()
         total = apply_far(
             jnp.zeros((leaves, leaf), F32), jnp.where(masks[0] > 0.0, chosen, 0.0), 0, local_levels
         )
@@ -164,10 +177,10 @@
             loads[5].wait()
         extended = jnp.concatenate([halo[step, 0], own[step], halo[step, 1]], axis=0)
         first_leaf = (me - 1) * leaves
-        spot = lax.broadcasted_iota(jnp.int32, (leaves, 3 * leaves), 1) + first_leaf
+        spot = lax.broadcasted_iota(jnp.int32, (3 * leaves, leaves), 0) + first_leaf
         for k in range(nears):
-            hot = (jnp.broadcast_to(index[:, k:k + 1], (leaves, 3 * leaves)) == spot)
-            picked = dot(hot.astype(F32).astype(BF16), extended, NN)
+            hot = jnp.broadcast_to(index[k:k + 1, :], (3 * leaves, leaves)) == spot
+            picked = dot(hot.astype(F32).astype(BF16), extended, TN)
             for i in range(leaves):
                 lhs = jnp.where(row == i, picked, 0.0).astype(BF16)
                 total += dot(lhs, near[i, k], NT)
@@ -231,12 +244,8 @@
     loads[0].wait()
     slip_rate = jnp.concatenate([slip[pl.ds(0, leaves, 2), :], slip[pl.ds(1, leaves, 2), :]], axis=1)
     first = product(0, slip_rate.astype(BF16).astype(F32))
-    first_out = pltpu.make_async_copy(out.at[0], first_hbm, out_sem.at[0])
-    first_out.start()
     relaxed = slip_rate + jnp.tanh(first / 3.0)
     product(1, relaxed.astype(BF16).astype(F32))
-    second_out = pltpu.make_async_copy(out.at[1], second_hbm, out_sem.at[1])
-    second_out.start()
 
     for step in range(2):
         for side in range(2):
@@ -248,8 +257,14 @@
             got_far.at[step, pl.ds(1, groups - 1)], got_far.at[step, pl.ds(1, groups - 1)],
             far_send.at[step],
         ).wait()
-    first_out.wait()
-    second_out.wait()
+
+
+def write(out, first, second, sem):
+    copies = [pltpu.make_async_copy(out.at[n], ref, sem.at[n]) for n, ref in enumerate((first, second))]
+    for copy in copies:
+        copy.start()
+    for copy in copies:
+        copy.wait()
 
 
 def local(count, slip_rate, near_blocks, near_index, far_left, far_right, far_ranks):
@@ -261,19 +276,18 @@
     assert leaf == 2 * LANES and 4 * rank == LANES and 2**cross == count
     flat = (patches // LANES, LANES)
     anywhere = pl.BlockSpec(memory_space=pl.ANY)
-    first, second = pl.pallas_call(
+    out = pl.pallas_call(
         functools.partial(kernel, (count, leaves, nears, leaf, levels, rank)),
-        out_shape=[jax.ShapeDtypeStruct(flat, F32)] * 2,
+        out_shape=pltpu.VMEM((2,) + flat, F32),
         in_specs=[anywhere] * 6,
-        out_specs=[anywhere] * 2,
+        out_specs=pl.BlockSpec(memory_space=pltpu.VMEM),
         scratch_shapes=[
             pltpu.VMEM(flat, F32),
             pltpu.VMEM(far_ranks.shape, jnp.int32),
-            pltpu.VMEM(near_index.shape, jnp.int32),
+            pltpu.VMEM(near_index.shape[::-1], jnp.int32),
             pltpu.VMEM(far_right.shape, BF16),
             pltpu.VMEM(near_blocks.shape, BF16),
             pltpu.VMEM(far_left.shape, BF16),
-            pltpu.VMEM((2,) + flat, F32),
             pltpu.VMEM((2, leaves, leaf), BF16),
             pltpu.VMEM((2, 2, leaves, leaf), BF16),
             pltpu.VMEM((-(-levels * rank // LANES), leaves, LANES), F32),
@@ -281,8 +295,8 @@
             pltpu.VMEM((2, plane, 1, LANES), F32),
             pltpu.VMEM((2, 1, LANES), F32),
             pltpu.VMEM((2, groups, 1, LANES), F32),
-            pltpu.SemaphoreType.DMA((7,)),
-            pltpu.SemaphoreType.DMA((2,)),
+            pltpu.SemaphoreType.DMA((6,)),
+            pltpu.SemaphoreType.DMA((PIECES,)),
             pltpu.SemaphoreType.DMA((2, 2)),
             pltpu.SemaphoreType.DMA((2, 2)),
             pltpu.SemaphoreType.DMA((2,)),
@@ -292,7 +306,15 @@
         ],
         compiler_params=pltpu.CompilerParams(collective_id=0, has_side_effects=True),
         name="hmatrix",
-    )(slip_rate.reshape(flat), far_ranks, near_index, far_right, near_blocks, far_left)
+    )(slip_rate.reshape(flat), far_ranks, near_index.T, far_right, near_blocks, far_left)
+    first, second = pl.pallas_call(
+        write,
+        out_shape=[jax.ShapeDtypeStruct(flat, F32)] * 2,
+        in_specs=[pl.BlockSpec(memory_space=pltpu.VMEM)],
+        out_specs=[anywhere] * 2,
+        scratch_shapes=[pltpu.SemaphoreType.DMA((2,))],
+        name="write",
+    )(pltpu.with_memory_space_constraint(out, pltpu.VMEM))
     return first.reshape(-1), second.reshape(-1)
 
 

time: 55.3 us -> 50.9 us (0.920)
  local copies, waits for them, and re-layouts: 4 us -> 0 us
    unnamed x3 -> x0, local copies, waits for them, and re-layouts: 4 us -> none
    pallas_call x1, Pallas kernels: 50.2 us -> 49.4 us  [local(): pl.pallas_call(functools.partial(kernel, (count, leaves, nears, leaf, lev...]
    pallas_call x0 -> x1, Pallas kernels: none -> 0.63 us  [local(): pl.pallas_call(write, out_shape=[jax.ShapeDtypeStruct(flat, F32)] * 2, in...]
where the time goes in v2:
time: 50.9 us; the launch traced here: 50.6 us
  Pallas kernels  50 us (98%)
  between operations  0.64 us (1%)
    pallas_call x1, Pallas kernels, local(): pl.pallas_call(functools.partial(kernel, (count, leaves, nears, leaf, lev...  49.4 us

profile of v2, /device:TPU:33, one launch (start us, length us, event | category | flops | bytes accessed | tf_op | source)
XLA Modules:
  0.0 50.6 jit_solution(1737746278645401528)
XLA Ops:
  0.6 49.4 %hmatrix.1.out = f32[2,32,128]{2,1,0:T(8,128)S(1)} custom-call(f32[32,128]{1,0:T(8,128)} %bitcast.4, s32[16,11]{1,0:T(8,128)} %ranks_hbm.1, s32[3,16]{1,0:T(4,128)} %bitcast.5, bf16[11,32,4096]{2,1,0:T(8,128)(2,1)} %right_hbm.1, bf16[16,3,256,256]{3,2,1,0:T(8,128)(2,1)} %near_hbm.1, bf16[11,32,4096]{2,1,0:T(8,128)(2,1)} %left_hbm.1), custom_call_target="tpu_custom_call" | custom-call | tf_op jit(solution)/shard_map/hmatrix/pallas_call | solution.py:279
  50.0 0.6 %write.1 = (f32[32,128]{1,0:T(8,128)}, f32[32,128]{1,0:T(8,128)}) custom-call(f32[2,32,128]{2,1,0:T(8,128)S(1)} %hmatrix.1.out), custom_call_target="tpu_custom_call" | custom-call | tf_op jit(solution)/shard_map/write/pallas_call | solution.py:310

commit v3 on v2

v3 whole, which is shorter than its diff:
```python
import functools
import math

import jax
import jax.numpy as jnp
from jax import lax
from jax.experimental import pallas as pl
from jax.experimental.pallas import tpu as pltpu
from jax.sharding import PartitionSpec as P

MESH = pl.DeviceIdType.MESH
F32 = jnp.float32
BF16 = jnp.bfloat16
LANES = 128
FAR_BITS = 2
PIECES = 4
NEAR_UNROLL = 4
NT = (((1,), (1,)), ((), ()))
NN = (((1,), (0,)), ((), ()))
TN = (((0,), (0,)), ((), ()))


def dot(a, b, dims):
    return lax.dot_general(a, b, dims, preferred_element_type=F32)


def add_all(terms):
    terms = list(terms)
    while len(terms) > 1:
        odd = terms[len(terms) // 2 * 2:]
        terms = [x + y for x, y in zip(terms[::2], terms[1::2])] + odd
    return terms[0]


def kernel(
    shape,
    slip_hbm, ranks_hbm, index_hbm, right_hbm, near_hbm, left_hbm,
    out,
    slip, ranks, index, right, near, left, own, halo, masks, picks, sums,
    mail, got, known, relay, got_relay, plane_sums, got_plane, got_all, got_pair,
    load_sem, piece_sem, halo_send, halo_recv, level_send, level_recv, relay_send, relay_recv,
    plane_send, plane_recv, all_send, all_recv, pair_send, pair_recv, ready, near_ready,
):
    count, leaves, nears, leaf, levels, rank = shape
    local_levels = leaves.bit_length() - 1
    cross = levels - local_levels
    groups = 2**FAR_BITS
    plane = count // groups
    ring_bits = cross - FAR_BITS - 1
    ring = 2**ring_bits
    me = lax.axis_index("leaf")
    spot = lax.rem(me // 2, ring)

    def peer_of(far, step, core):
        return jnp.bitwise_xor(me, far * plane + step * 2 + core)

    def bit(j):
        return lax.rem(spot // 2**j, 2) == 1

    def target(peer):
        return dict(device_id={"leaf": peer}, device_id_type=MESH)

    right_of = lax.rem(me + 1, count)
    left_of = lax.rem(me + count - 1, count)
    far_first = [g for g in (2, 3, 1, 0) if g < groups]
    quad_bits = ring_bits - 2
    quad = 2 ** (quad_bits + 1)
    upper = range(quad_bits, ring_bits)
    relay_step = {quad_bits: ring // 4, quad_bits + 1: ring // 2 + ring // 4}
    half = ring // 2
    runs = [(ring_bits - 1, half, 1, half // 2), (ring_bits - 2, half - 1, -1, half // 2),
            (ring_bits - 1, half + half // 2, 1, half // 2)]
    runs += [(j, 2 ** (j + 1) - 1, -1, 2**j) for j in reversed(range(ring_bits - 2))]

    def run(first, stride, length, body):
        def trip(n, carry):
            body(first + stride * n)
            return carry

        lax.fori_loop(0, length, trip, 0)

    high = local_levels - 1
    piece = leaves // PIECES * leaf
    loads = [
        pltpu.make_async_copy(slip_hbm, slip, load_sem.at[0]),
        pltpu.make_async_copy(left_hbm, left, load_sem.at[1]),
        pltpu.make_async_copy(ranks_hbm, ranks, load_sem.at[2]),
        pltpu.make_async_copy(index_hbm, index, load_sem.at[3]),
        pltpu.make_async_copy(right_hbm.at[pl.ds(0, high)], right.at[pl.ds(0, high)], load_sem.at[4]),
        pltpu.make_async_copy(near_hbm, near, load_sem.at[5]),
    ]
    pieces = []
    for n in range(PIECES):
        part = (pl.ds(high, levels - high), slice(None), pl.ds(n * piece, piece))
        pieces.append(pltpu.make_async_copy(right_hbm.at[part], right.at[part], piece_sem.at[n]))
    loads[0].start()
    for load in pieces:
        load.start()

    barrier = pltpu.get_barrier_semaphore()

    def greet(peer):
        pl.semaphore_signal(barrier, inc=1, **target(peer))

    expected = quad - 1 + groups - 1
    for j, first_step, stride, length in runs:
        if j > quad_bits:
            @pl.when(jnp.logical_not(bit(j)))
            def _(first_step=first_step, stride=stride, length=length):
                def both(step):
                    for c in range(2):
                        greet(peer_of(0, step, c))
                run(first_step, stride, length, both)
    pl.when(bit(quad_bits))(lambda: greet(peer_of(0, relay_step[quad_bits], 0)))
    for t in reversed(range(1, quad)):
        greet(peer_of(0, t // 2, t % 2))
    for g in far_first[:-1]:
        greet(peer_of(g, 0, 0))
    top = jnp.logical_and(spot == ring - 1, lax.rem(me, 2) == 1)
    bottom = jnp.logical_and(spot == 0, lax.rem(me, 2) == 0)
    pl.when(jnp.logical_not(top))(lambda: greet(right_of))
    pl.when(bottom)(lambda: greet(left_of))
    expected = expected + jnp.where(bottom, 0, 1) + jnp.where(top, 1, 0)
    for j in upper:
        expected = expected + (
            jnp.where(bit(j), 2 ** (j + 1), 0) if j > quad_bits else jnp.where(bit(j), 0, 1)
        )
    for load in (loads[2], loads[3], loads[4], loads[1], loads[5]):
        load.start()

    row = lax.broadcasted_iota(jnp.int32, (leaves, leaf), 0)
    row_l = lax.broadcasted_iota(jnp.int32, (leaves, LANES), 0)
    lane = lax.broadcasted_iota(jnp.int32, (leaves, LANES), 1)
    lane1 = lax.broadcasted_iota(jnp.int32, (1, LANES), 1)

    def scale_of(level):
        return 1.0 / math.sqrt(leaf * 2**level)

    def by_lane(values):
        scale = jnp.zeros((1, LANES), F32)
        for part, value in enumerate(values):
            scale = jnp.where(lane1 // rank == part, value, scale)
        return scale

    def project(vf, start, stop, ready=()):
        rows = (stop - start) * rank
        @pl.when(spot >= 0)
        def _():
            totals = [jnp.zeros((leaves, rows), F32)] * 2
            for c in range(leaves):
                if ready and c % (leaves // PIECES) == 0:
                    ready[c // (leaves // PIECES)].wait()
                lhs = jnp.where(row == c, vf, 0.0).astype(BF16)
                rhs = right[start:stop, :, c * leaf:(c + 1) * leaf].reshape(rows, leaf)
                totals[c % 2] += dot(lhs, rhs, NT)
            for n in range(2):
                sums[n, :, :rows] = totals[n]

        return sums[0, :, :rows] + sums[1, :, :rows]

    def apply_far(total, weights, start, stop):
        rows = (stop - start) * rank
        row_w = lax.broadcasted_iota(jnp.int32, weights.shape, 0)

        @pl.when(spot >= 0)
        def _():
            totals = [jnp.zeros((leaves, leaf), F32)] * 2
            for i in range(leaves):
                lhs = jnp.where(row_w == i, weights, 0.0).astype(BF16)[:, :rows]
                rhs = left[start:stop, :, i * leaf:(i + 1) * leaf].reshape(rows, leaf)
                totals[i % 2] += dot(lhs, rhs, NN)
            for n in range(2):
                sums[n] = totals[n]

        return sums[0] + sums[1] if total is None else total + sums[0] + sums[1]

    def spread(mask, value):
        return jnp.where(masks[mask] > 0.0, jnp.broadcast_to(value, (leaves, LANES)), 0.0)

    def send(src, dst, send_sem, recv_sem, peer):
        pltpu.make_async_remote_copy(
            src_ref=src, dst_ref=dst, send_sem=send_sem, recv_sem=recv_sem, **target(peer)
        ).start()

    def rows_done(ref, rows, sem):
        part = ref.at[pl.ds(0, rows)]
        pltpu.make_async_copy(part, part, sem).wait()

    def write_mail(step, vf, ready=()):
        own[step] = vf.astype(BF16)
        summed = project(vf, high, levels, ready)
        device_sums = jnp.sum(summed, axis=0, keepdims=True)
        one = pltpu.roll(device_sums[:, :LANES], 2 * rank, 1)
        two = pltpu.roll(device_sums[:, LANES:], 2 * rank, 1)
        mail[step, 0] = jnp.where(lane1 < 2 * rank, one, two)
        mail[step, 1] = jnp.where(lane1 < 2 * rank, two, one)
        return summed[:, :rank]

    def send_halo(step, side):
        send(own.at[step], halo.at[step, side], halo_send.at[step, side], halo_recv.at[step, side],
             left_of if side else right_of)

    def wait_halo(step, sems):
        for side in range(2):
            pltpu.make_async_copy(own.at[step], own.at[step], sems.at[step, side]).wait()

    def far_slot(g, step, c):
        return g * plane + step * 2 + c

    def local_part(step, vf, last_local, pair):
        below = project(vf, 0, high)
        fine = jnp.concatenate([below, last_local], axis=1)
        chosen = jnp.zeros((leaves, LANES), F32)
        cluster_r = lax.broadcasted_iota(jnp.int32, (leaves, leaves), 0)
        cluster_c = lax.broadcasted_iota(jnp.int32, (leaves, leaves), 1)
        for level in range(local_levels):
            pick = (cluster_c >> level) == ((cluster_r >> level) ^ 1)
            partner = lax.dot_general(
                pick.astype(F32), fine, NN,
                precision=lax.Precision.HIGHEST, preferred_element_type=F32,
            )
            chosen = jnp.where(lane // rank == level, partner * scale_of(level), chosen)
        chosen = jnp.where(masks[0] > 0.0, chosen, 0.0)
        pair = pltpu.roll(spread(2, pair * scale_of(local_levels)), rank, 1)
        total = apply_far(None, jnp.concatenate([chosen, pair], axis=1), 0, local_levels + 1)
        wait_halo(step, halo_recv)
        extended = jnp.concatenate([halo[step, 0], own[step], halo[step, 1]], axis=0)
        leaf_no = lax.broadcasted_iota(jnp.int32, (3 * leaves, leaves), 0) + (me - 1) * leaves
        for k in range(nears):
            hot = jnp.broadcast_to(index[k:k + 1, :], (3 * leaves, leaves)) == leaf_no
            picks[k] = dot(hot.astype(F32).astype(BF16), extended, TN)

        def near_leaves(n, totals):
            totals = list(totals)
            for m in range(NEAR_UNROLL):
                i = n * NEAR_UNROLL + m
                for k in range(nears):
                    lhs = jnp.where(row == i, picks[k], 0.0).astype(BF16)
                    totals[m % 2] += dot(lhs, near[i, k], NT)
            return tuple(totals)

        totals = lax.fori_loop(
            0, leaves // NEAR_UNROLL, near_leaves, (total, jnp.zeros((leaves, leaf), F32))
        )
        return totals[0] + totals[1]

    ring_scale = by_lane([scale_of(local_levels + 1 + j) for j in range(ring_bits)])
    plane_scale = by_lane([scale_of(levels - 2), scale_of(levels - 1)])
    ring_levels = (local_levels + 1, local_levels + 1 + ring_bits)

    def finish(step, total):
        out[step, pl.ds(0, leaves, 2), :] = total[:, :LANES]
        out[step, pl.ds(1, leaves, 2), :] = total[:, LANES:]

    loads[0].wait()
    slip_rate = jnp.concatenate([slip[pl.ds(0, leaves, 2), :], slip[pl.ds(1, leaves, 2), :]], axis=1)
    vf = slip_rate.astype(BF16).astype(F32)
    last_local = write_mail(0, vf, pieces)
    pl.semaphore_wait(barrier, expected)
    for j in upper:
        @pl.when(bit(j) if j > quad_bits else jnp.logical_not(bit(j)))
        def _(j=j):
            pl.semaphore_signal(ready.at[j - quad_bits], inc=1, **target(peer_of(0, relay_step[j], 0)))

    pl.when(jnp.logical_not(bottom))(
        lambda: pl.semaphore_signal(near_ready.at[0], inc=1, **target(left_of)))
    pl.when(top)(lambda: pl.semaphore_signal(near_ready.at[1], inc=1, **target(right_of)))

    def send_letter(t, sem):
        send(mail.at[0], got.at[t], level_send.at[sem], level_recv.at[sem], jnp.bitwise_xor(me, t))

    for t in reversed(range(1, quad)):
        send_letter(t, 1)
    for j, first_step, stride, length in runs:
        if j > quad_bits:
            @pl.when(bit(j))
            def _(j=j, first_step=first_step, stride=stride, length=length):
                def both(step):
                    for c in range(2):
                        send_letter(step * 2 + c, 0)
                run(first_step, stride, length, both)
    pl.when(jnp.logical_not(top))(lambda: pl.semaphore_wait(near_ready.at[0], 1))
    send_halo(0, 0)
    pl.when(jnp.logical_not(bottom))(lambda: send_halo(0, 1))

    rows_done(got, quad - 1, level_recv.at[1])

    def sum_of(j, kind):
        return add_all(got[t, kind] for t in range(2 ** (j + 1), 2 ** (j + 2)))

    quad_ring = [sum_of(j, 0) for j in range(quad_bits)]
    known[0] = add_all([mail[0, 0], got[1, 0]] + quad_ring)
    known[1] = add_all([mail[0, 1], got[1, 1]] + [sum_of(j, 1) for j in range(quad_bits)])
    given = jnp.zeros((1, LANES), F32)
    for j in range(quad_bits):
        given = jnp.where(lane1 // rank == j, quad_ring[j], given)
    known[2] = given

    def take(j, ring_sum, far_sum):
        known[2] = jnp.where(lane1 // rank == j, ring_sum, known[2])
        known[0] = known[0] + ring_sum
        known[1] = known[1] + far_sum

    def settle_relay(n):
        part = got_relay.at[n]
        pltpu.make_async_copy(part, part, relay_recv.at[n]).wait()
        take(quad_bits + n, got_relay[n, 0], got_relay[n, 1])

    def send_relay(n):
        relay[n, 0] = known[0]
        relay[n, 1] = known[1]
        waits = jnp.logical_not(bit(quad_bits + n)) if n else bit(quad_bits)
        pl.when(waits)(lambda: pl.semaphore_wait(ready.at[n], 1))
        send(relay.at[n], got_relay.at[n], relay_send.at[n], relay_recv.at[n],
             peer_of(0, relay_step[quad_bits + n], 0))

    send_relay(0)
    low = jnp.logical_not(bit(ring_bits - 1))

    @pl.when(bottom)
    def _():
        pl.semaphore_wait(near_ready.at[1], 1)
        send_halo(0, 1)

    @pl.when(low)
    def _():
        settle_relay(0)
        send_relay(1)

    loads[2].wait()
    loads[3].wait()
    for group, held in enumerate((
        list(range(local_levels)), list(range(*ring_levels)),
        [levels - 2, levels - 1, None, local_levels],
    )):
        limit = jnp.zeros((leaves, LANES), jnp.int32)
        for part, level in enumerate(held):
            if level is not None:
                column = jnp.broadcast_to(ranks[:, level:level + 1], (leaves, LANES))
                limit = jnp.where(lane // rank == part, column, limit)
        masks[group] = (lane % rank < limit).astype(F32)
    for n in (4, 1, 5):
        loads[n].wait()
    total = local_part(0, vf, last_local, got[1, 1])
    @pl.when(jnp.logical_not(low))
    def _():
        settle_relay(0)
        settle_relay(1)

    @pl.when(low)
    def _():
        rows_done(got, ring, level_recv.at[0])
        take(ring_bits - 1, sum_of(ring_bits - 1, 0), sum_of(ring_bits - 1, 1))

    plane_sums[...] = known[1]
    for g in far_first[:-1]:
        send(plane_sums, got_plane.at[g], plane_send.at[0], plane_recv.at[0], peer_of(g, 0, 0))
    total = apply_far(total, spread(1, known[2] * ring_scale), *ring_levels)
    rows_done(got_plane, groups - 1, plane_recv.at[0])
    far_sum = jnp.where(lane1 < rank, got_plane[1], add_all(got_plane[g] for g in range(2, groups)))
    first = apply_far(total, spread(2, far_sum * plane_scale), levels - FAR_BITS, levels)
    finish(0, first)

    relaxed = slip_rate + jnp.tanh(first / 3.0)
    vf = relaxed.astype(BF16).astype(F32)
    last_local = write_mail(1, vf)
    def send_row(g, step, c):
        sem = 1 if g else 0
        slot = g * plane + step * 2 + c
        send(mail.at[1, sem], got_all.at[slot], all_send.at[sem], all_recv.at[sem], peer_of(g, step, c))

    for j, first_step, stride, length in runs:
        def all_of(step):
            for g in far_first:
                for c in range(2):
                    send_row(g, step, c)
        run(first_step, stride, length, all_of)
    for g in far_first[:-1]:
        for c in range(2):
            send_row(g, 0, c)
    send(mail.at[1, 1], got_pair, pair_send.at[0], pair_recv.at[0], peer_of(0, 0, 1))
    send_halo(1, 0)
    send_halo(1, 1)
    pltpu.make_async_copy(got_pair, got_pair, pair_recv.at[0]).wait()
    total = local_part(1, vf, last_local, got_pair[...])
    rows_done(got_all, plane - 2, all_recv.at[0])
    sibling = jnp.zeros((1, LANES), F32)
    for j in range(ring_bits):
        ring_sum = add_all(got_all[t] for t in range(2 ** (j + 1), 2 ** (j + 2)))
        sibling = jnp.where(lane1 // rank == j, ring_sum, sibling)
    total = apply_far(total, spread(1, sibling * ring_scale), *ring_levels)
    rows_done(got_all, count - plane, all_recv.at[1])
    far_sum = jnp.where(
        lane1 < rank, add_all(got_all[t] for t in range(plane, 2 * plane)),
        add_all(got_all[t] for t in range(2 * plane, count)),
    )
    finish(1, apply_far(total, spread(2, far_sum * plane_scale), levels - FAR_BITS, levels))

    for step in range(2):
        wait_halo(step, halo_send)
    rows_done(got, quad - 1, level_send.at[1])
    pltpu.make_async_copy(relay.at[0], relay.at[0], relay_send.at[0]).wait()

    @pl.when(low)
    def _():
        pltpu.make_async_copy(relay.at[1], relay.at[1], relay_send.at[1]).wait()

    @pl.when(jnp.logical_not(low))
    def _():
        rows_done(got, ring, level_send.at[0])

    rows_done(got_plane, groups - 1, plane_send.at[0])
    rows_done(got_all, plane - 2, all_send.at[0])
    rows_done(got_all, count - plane, all_send.at[1])
    pltpu.make_async_copy(got_pair, got_pair, pair_send.at[0]).wait()


def write(out, first, second, sem):
    copies = [pltpu.make_async_copy(out.at[n], ref, sem.at[n]) for n, ref in enumerate((first, second))]
    for copy in copies:
        copy.start()
    for copy in copies:
        copy.wait()


def local(count, slip_rate, near_blocks, near_index, far_left, far_right, far_ranks):
    leaves, nears, leaf, _ = near_blocks.shape
    levels, rank, patches = far_left.shape
    cross = levels - (leaves.bit_length() - 1)
    ring_bits = cross - FAR_BITS - 1
    plane = count // 2**FAR_BITS
    assert leaf == 2 * LANES and 4 * rank == LANES and 2**cross == count
    assert leaves == 16 and ring_bits == 4
    flat = (patches // LANES, LANES)
    anywhere = pl.BlockSpec(memory_space=pl.ANY)
    dma = pltpu.SemaphoreType.DMA
    out = pl.pallas_call(
        functools.partial(kernel, (count, leaves, nears, leaf, levels, rank)),
        out_shape=pltpu.VMEM((2,) + flat, F32),
        in_specs=[anywhere] * 6,
        out_specs=pl.BlockSpec(memory_space=pltpu.VMEM),
        scratch_shapes=[
            pltpu.VMEM(flat, F32),
            pltpu.VMEM(far_ranks.shape, jnp.int32),
            pltpu.VMEM(near_index.shape[::-1], jnp.int32),
            pltpu.VMEM(far_right.shape, BF16),
            pltpu.VMEM(near_blocks.shape, BF16),
            pltpu.VMEM(far_left.shape, BF16),
            pltpu.VMEM((2, leaves, leaf), BF16),
            pltpu.VMEM((2, 2, leaves, leaf), BF16),
            pltpu.VMEM((3, leaves, LANES), F32),
            pltpu.VMEM((nears, leaves, leaf), F32),
            pltpu.VMEM((2, leaves, leaf), F32),
            pltpu.VMEM((2, 2, 1, LANES), F32),
            pltpu.VMEM((plane, 2, 1, LANES), F32),
            pltpu.VMEM((3, 1, LANES), F32),
            pltpu.VMEM((2, 2, 1, LANES), F32),
            pltpu.VMEM((2, 2, 1, LANES), F32),
            pltpu.VMEM((1, LANES), F32),
            pltpu.VMEM((2**FAR_BITS, 1, LANES), F32),
            pltpu.VMEM((count, 1, LANES), F32),
            pltpu.VMEM((1, LANES), F32),
            dma((6,)), dma((PIECES,)), dma((2, 2)), dma((2, 2)),
            dma((2,)), dma((2,)), dma((2,)), dma((2,)),
            dma((1,)), dma((1,)), dma((2,)), dma((2,)), dma((1,)), dma((1,)),
            pltpu.SemaphoreType.REGULAR((2,)), pltpu.SemaphoreType.REGULAR((2,)),
        ],
        compiler_params=pltpu.CompilerParams(collective_id=0, has_side_effects=True),
        name="hmatrix",
    )(slip_rate.reshape(flat), far_ranks, near_index.T, far_right, near_blocks, far_left)
    first, second = pl.pallas_call(
        write,
        out_shape=[jax.ShapeDtypeStruct(flat, F32)] * 2,
        in_specs=[pl.BlockSpec(memory_space=pltpu.VMEM)],
        out_specs=[anywhere] * 2,
        scratch_shapes=[dma((2,))],
        name="write",
    )(pltpu.with_memory_space_constraint(out, pltpu.VMEM))
    return first.reshape(-1), second.reshape(-1)


def solution(mesh):
    both = ("models", "leaf")
    in_specs = (
        P(both), P(both, None, None, None), P(both, None),
        P(None, None, both), P(None, None, both), P(both, None),
    )
    return jax.shard_map(
        functools.partial(local, mesh.shape["leaf"]), mesh=mesh, in_specs=in_specs,
        out_specs=(P(both), P(both)), check_vma=False,
    )
```

time: 50.9 us -> 49.1 us (0.965)
  Pallas kernels: 50 us -> 48.3 us
    pallas_call x1, Pallas kernels: 49.4 us -> 47.7 us  [local(): pl.pallas_call(functools.partial(kernel, (count, leaves, nears, leaf, lev...]
where the time goes in v3:
time: 49.1 us; the launch traced here: 49 us
  Pallas kernels  48.3 us (98%)
  between operations  0.64 us (1%)
    pallas_call x1, Pallas kernels, local(): pl.pallas_call(functools.partial(kernel, (count, leaves, nears, leaf, lev...  47.7 us

profile of v3, /device:TPU:33, one launch (start us, length us, event | category | flops | bytes accessed | tf_op | source)
XLA Modules:
  0.0 49.0 jit_solution(2543246487019888669)
XLA Ops:
  0.6 47.7 %hmatrix.1.out = f32[2,32,128]{2,1,0:T(8,128)S(1)} custom-call(f32[32,128]{1,0:T(8,128)} %bitcast.4, s32[16,11]{1,0:T(8,128)} %ranks_hbm.1, s32[3,16]{1,0:T(4,128)} %bitcast.5, bf16[11,32,4096]{2,1,0:T(8,128)(2,1)} %right_hbm.1, bf16[16,3,256,256]{3,2,1,0:T(8,128)(2,1)} %near_hbm.1, bf16[11,32,4096]{2,1,0:T(8,128)(2,1)} %left_hbm.1), custom_call_target="tpu_custom_call" | custom-call | tf_op jit(solution)/shard_map/hmatrix/pallas_call | solution.py:437
  48.3 0.6 %write.1 = (f32[32,128]{1,0:T(8,128)}, f32[32,128]{1,0:T(8,128)}) custom-call(f32[2,32,128]{2,1,0:T(8,128)S(1)} %hmatrix.1.out), custom_call_target="tpu_custom_call" | custom-call | tf_op jit(solution)/shard_map/write/pallas_call | solution.py:471

commit v4 on v3

--- a/solution.py
+++ b/solution.py
@@ -36,10 +36,10 @@
     shape,
     slip_hbm, ranks_hbm, index_hbm, right_hbm, near_hbm, left_hbm,
     out,
-    slip, ranks, index, right, near, left, own, halo, masks, picks, sums,
+    slip, ranks, index, right, near, left, own, halo, masks, picks, sums, partial,
     mail, got, known, relay, got_relay, plane_sums, got_plane, got_all, got_pair,
     load_sem, piece_sem, halo_send, halo_recv, level_send, level_recv, relay_send, relay_recv,
-    plane_send, plane_recv, all_send, all_recv, pair_send, pair_recv, ready, near_ready,
+    plane_send, plane_recv, all_send, all_recv, pair_send, pair_recv, ready, near_ready, plane_ready,
 ):
     count, leaves, nears, leaf, levels, rank = shape
     local_levels = leaves.bit_length() - 1
@@ -102,29 +102,40 @@
     def greet(peer):
         pl.semaphore_signal(barrier, inc=1, **target(peer))
 
-    expected = quad - 1 + groups - 1
+    low = jnp.logical_not(bit(ring_bits - 1))
+    outer = bit(ring_bits - 1) == bit(quad_bits)
+    inner = jnp.logical_not(outer)
+    plane_no = me // plane
+
+    def plane_above(g):
+        return lax.rem(plane_no // 2 ** (g.bit_length() - 1), 2) == 1
+
     for j, first_step, stride, length in runs:
         if j > quad_bits:
-            @pl.when(jnp.logical_not(bit(j)))
+            @pl.when(low)
             def _(first_step=first_step, stride=stride, length=length):
                 def both(step):
                     for c in range(2):
                         greet(peer_of(0, step, c))
                 run(first_step, stride, length, both)
-    pl.when(bit(quad_bits))(lambda: greet(peer_of(0, relay_step[quad_bits], 0)))
+    expected = quad - 1
     for t in reversed(range(1, quad)):
         greet(peer_of(0, t // 2, t % 2))
     for g in far_first[:-1]:
-        greet(peer_of(g, 0, 0))
+        pl.when(plane_above(g))(lambda g=g: greet(peer_of(g, 0, 0)))
+        expected = expected + jnp.where(plane_above(g), 0, 1)
+    @pl.when(inner)
+    def _():
+        for t in reversed(range(quad, 2 * quad)):
+            greet(peer_of(0, t // 2, t % 2))
+
+    expected = expected + jnp.where(outer, quad, 0)
+    expected = expected + jnp.where(low, 0, ring)
     top = jnp.logical_and(spot == ring - 1, lax.rem(me, 2) == 1)
     bottom = jnp.logical_and(spot == 0, lax.rem(me, 2) == 0)
     pl.when(jnp.logical_not(top))(lambda: greet(right_of))
     pl.when(bottom)(lambda: greet(left_of))
     expected = expected + jnp.where(bottom, 0, 1) + jnp.where(top, 1, 0)
-    for j in upper:
-        expected = expected + (
-            jnp.where(bit(j), 2 ** (j + 1), 0) if j > quad_bits else jnp.where(bit(j), 0, 1)
-        )
     for load in (loads[2], loads[3], loads[4], loads[1], loads[5]):
         load.start()
 
@@ -207,7 +218,7 @@
     def far_slot(g, step, c):
         return g * plane + step * 2 + c
 
-    def local_part(step, vf, last_local, pair):
+    def local_part(step, vf, last_local):
         below = project(vf, 0, high)
         fine = jnp.concatenate([below, last_local], axis=1)
         chosen = jnp.zeros((leaves, LANES), F32)
@@ -221,8 +232,7 @@
             )
             chosen = jnp.where(lane // rank == level, partner * scale_of(level), chosen)
         chosen = jnp.where(masks[0] > 0.0, chosen, 0.0)
-        pair = pltpu.roll(spread(2, pair * scale_of(local_levels)), rank, 1)
-        total = apply_far(None, jnp.concatenate([chosen, pair], axis=1), 0, local_levels + 1)
+        total = apply_far(None, chosen, 0, local_levels)
         wait_halo(step, halo_recv)
         extended = jnp.concatenate([halo[step, 0], own[step], halo[step, 1]], axis=0)
         leaf_no = lax.broadcasted_iota(jnp.int32, (3 * leaves, leaves), 0) + (me - 1) * leaves
@@ -242,7 +252,13 @@
         totals = lax.fori_loop(
             0, leaves // NEAR_UNROLL, near_leaves, (total, jnp.zeros((leaves, leaf), F32))
         )
-        return totals[0] + totals[1]
+        partial[...] = totals[0] + totals[1]
+
+    def apply_ring(pair, siblings):
+        pair = pltpu.roll(spread(2, pair * scale_of(local_levels)), rank, 1)
+        moved = pltpu.roll(spread(1, siblings * ring_scale), rank, 1)
+        weights = jnp.concatenate([jnp.where(lane < rank, pair, moved), moved], axis=1)
+        return apply_far(partial[...], weights, local_levels, local_levels + 1 + ring_bits)
 
     ring_scale = by_lane([scale_of(local_levels + 1 + j) for j in range(ring_bits)])
     plane_scale = by_lane([scale_of(levels - 2), scale_of(levels - 1)])
@@ -252,25 +268,38 @@
         out[step, pl.ds(0, leaves, 2), :] = total[:, :LANES]
         out[step, pl.ds(1, leaves, 2), :] = total[:, LANES:]
 
+    def meet():
+        pl.semaphore_wait(barrier, expected)
+        for j in upper:
+            @pl.when(bit(j) if j > quad_bits else outer)
+            def _(j=j):
+                pl.semaphore_signal(ready.at[j - quad_bits], inc=1, **target(peer_of(0, relay_step[j], 0)))
+
+        for g in far_first[:-1]:
+            pl.when(jnp.logical_not(plane_above(g)))(
+                lambda g=g: pl.semaphore_signal(plane_ready.at[g], inc=1, **target(peer_of(g, 0, 0))))
+        pl.when(jnp.logical_not(bottom))(
+            lambda: pl.semaphore_signal(near_ready.at[0], inc=1, **target(left_of)))
+        pl.when(top)(lambda: pl.semaphore_signal(near_ready.at[1], inc=1, **target(right_of)))
+
+    last = spot == ring - 1
+    late = spot >= ring - ring // 4
+    pl.when(last)(meet)
     loads[0].wait()
     slip_rate = jnp.concatenate([slip[pl.ds(0, leaves, 2), :], slip[pl.ds(1, leaves, 2), :]], axis=1)
     vf = slip_rate.astype(BF16).astype(F32)
     last_local = write_mail(0, vf, pieces)
-    pl.semaphore_wait(barrier, expected)
-    for j in upper:
-        @pl.when(bit(j) if j > quad_bits else jnp.logical_not(bit(j)))
-        def _(j=j):
-            pl.semaphore_signal(ready.at[j - quad_bits], inc=1, **target(peer_of(0, relay_step[j], 0)))
-
-    pl.when(jnp.logical_not(bottom))(
-        lambda: pl.semaphore_signal(near_ready.at[0], inc=1, **target(left_of)))
-    pl.when(top)(lambda: pl.semaphore_signal(near_ready.at[1], inc=1, **target(right_of)))
-
+    pl.when(jnp.logical_not(last))(meet)
     def send_letter(t, sem):
         send(mail.at[0], got.at[t], level_send.at[sem], level_recv.at[sem], jnp.bitwise_xor(me, t))
 
     for t in reversed(range(1, quad)):
         send_letter(t, 1)
+    @pl.when(outer)
+    def _():
+        for t in reversed(range(quad, 2 * quad)):
+            send_letter(t, 2)
+
     for j, first_step, stride, length in runs:
         if j > quad_bits:
             @pl.when(bit(j))
@@ -283,6 +312,25 @@
     send_halo(0, 0)
     pl.when(jnp.logical_not(bottom))(lambda: send_halo(0, 1))
 
+    def own_work():
+        loads[2].wait()
+        loads[3].wait()
+        for group, held in enumerate((
+            list(range(local_levels)), list(range(*ring_levels)),
+            [levels - 2, levels - 1, None, local_levels],
+        )):
+            limit = jnp.zeros((leaves, LANES), jnp.int32)
+            for part, level in enumerate(held):
+                if level is not None:
+                    column = jnp.broadcast_to(ranks[:, level:level + 1], (leaves, LANES))
+                    limit = jnp.where(lane // rank == part, column, limit)
+            masks[group] = (lane % rank < limit).astype(F32)
+        for n in (4, 1, 5):
+            loads[n].wait()
+        local_part(0, vf, last_local)
+
+    pl.when(late)(own_work)
+
     rows_done(got, quad - 1, level_recv.at[1])
 
     def sum_of(j, kind):
@@ -309,42 +357,34 @@
     def send_relay(n):
         relay[n, 0] = known[0]
         relay[n, 1] = known[1]
-        waits = jnp.logical_not(bit(quad_bits + n)) if n else bit(quad_bits)
-        pl.when(waits)(lambda: pl.semaphore_wait(ready.at[n], 1))
+        pl.semaphore_wait(ready.at[n], 1)
         send(relay.at[n], got_relay.at[n], relay_send.at[n], relay_recv.at[n],
              peer_of(0, relay_step[quad_bits + n], 0))
 
-    send_relay(0)
-    low = jnp.logical_not(bit(ring_bits - 1))
+    pl.when(inner)(lambda: send_relay(0))
 
     @pl.when(bottom)
     def _():
         pl.semaphore_wait(near_ready.at[1], 1)
         send_halo(0, 1)
 
+    def settle_half():
+        pl.when(outer)(lambda: settle_relay(0))
+
+        @pl.when(inner)
+        def _():
+            rows_done(got, quad, level_recv.at[2])
+            take(quad_bits, sum_of(quad_bits, 0), sum_of(quad_bits, 1))
+
     @pl.when(low)
     def _():
-        settle_relay(0)
+        settle_half()
         send_relay(1)
 
-    loads[2].wait()
-    loads[3].wait()
-    for group, held in enumerate((
-        list(range(local_levels)), list(range(*ring_levels)),
-        [levels - 2, levels - 1, None, local_levels],
-    )):
-        limit = jnp.zeros((leaves, LANES), jnp.int32)
-        for part, level in enumerate(held):
-            if level is not None:
-                column = jnp.broadcast_to(ranks[:, level:level + 1], (leaves, LANES))
-                limit = jnp.where(lane // rank == part, column, limit)
-        masks[group] = (lane % rank < limit).astype(F32)
-    for n in (4, 1, 5):
-        loads[n].wait()
-    total = local_part(0, vf, last_local, got[1, 1])
+    pl.when(jnp.logical_not(late))(own_work)
     @pl.when(jnp.logical_not(low))
     def _():
-        settle_relay(0)
+        settle_half()
         settle_relay(1)
 
     @pl.when(low)
@@ -354,8 +394,9 @@
 
     plane_sums[...] = known[1]
     for g in far_first[:-1]:
+        pl.when(plane_above(g))(lambda g=g: pl.semaphore_wait(plane_ready.at[g], 1))
         send(plane_sums, got_plane.at[g], plane_send.at[0], plane_recv.at[0], peer_of(g, 0, 0))
-    total = apply_far(total, spread(1, known[2] * ring_scale), *ring_levels)
+    total = apply_ring(got[1, 1], known[2])
     rows_done(got_plane, groups - 1, plane_recv.at[0])
     far_sum = jnp.where(lane1 < rank, got_plane[1], add_all(got_plane[g] for g in range(2, groups)))
     first = apply_far(total, spread(2, far_sum * plane_scale), levels - FAR_BITS, levels)
@@ -381,14 +422,14 @@
     send(mail.at[1, 1], got_pair, pair_send.at[0], pair_recv.at[0], peer_of(0, 0, 1))
     send_halo(1, 0)
     send_halo(1, 1)
+    local_part(1, vf, last_local)
     pltpu.make_async_copy(got_pair, got_pair, pair_recv.at[0]).wait()
-    total = local_part(1, vf, last_local, got_pair[...])
     rows_done(got_all, plane - 2, all_recv.at[0])
     sibling = jnp.zeros((1, LANES), F32)
     for j in range(ring_bits):
         ring_sum = add_all(got_all[t] for t in range(2 ** (j + 1), 2 ** (j + 2)))
         sibling = jnp.where(lane1 // rank == j, ring_sum, sibling)
-    total = apply_far(total, spread(1, sibling * ring_scale), *ring_levels)
+    total = apply_ring(got_pair[...], sibling)
     rows_done(got_all, count - plane, all_recv.at[1])
     far_sum = jnp.where(
         lane1 < rank, add_all(got_all[t] for t in range(plane, 2 * plane)),
@@ -399,7 +440,9 @@
     for step in range(2):
         wait_halo(step, halo_send)
     rows_done(got, quad - 1, level_send.at[1])
-    pltpu.make_async_copy(relay.at[0], relay.at[0], relay_send.at[0]).wait()
+    pl.when(inner)(
+        lambda: pltpu.make_async_copy(relay.at[0], relay.at[0], relay_send.at[0]).wait())
+    pl.when(outer)(lambda: rows_done(got, quad, level_send.at[2]))
 
     @pl.when(low)
     def _():
@@ -451,6 +494,7 @@
             pltpu.VMEM((3, leaves, LANES), F32),
             pltpu.VMEM((nears, leaves, leaf), F32),
             pltpu.VMEM((2, leaves, leaf), F32),
+            pltpu.VMEM((leaves, leaf), F32),
             pltpu.VMEM((2, 2, 1, LANES), F32),
             pltpu.VMEM((plane, 2, 1, LANES), F32),
             pltpu.VMEM((3, 1, LANES), F32),
@@ -461,9 +505,10 @@
             pltpu.VMEM((count, 1, LANES), F32),
             pltpu.VMEM((1, LANES), F32),
             dma((6,)), dma((PIECES,)), dma((2, 2)), dma((2, 2)),
-            dma((2,)), dma((2,)), dma((2,)), dma((2,)),
+            dma((3,)), dma((3,)), dma((2,)), dma((2,)),
             dma((1,)), dma((1,)), dma((2,)), dma((2,)), dma((1,)), dma((1,)),
             pltpu.SemaphoreType.REGULAR((2,)), pltpu.SemaphoreType.REGULAR((2,)),
+            pltpu.SemaphoreType.REGULAR((2**FAR_BITS,)),
         ],
         compiler_params=pltpu.CompilerParams(collective_id=0, has_side_effects=True),
         name="hmatrix",

time: 49.1 us -> 47.2 us (0.961)
  Pallas kernels: 48.3 us -> 46.4 us
    pallas_call x1, Pallas kernels: 47.7 us -> 45.8 us  [local(): pl.pallas_call(functools.partial(kernel, (count, leaves, nears, leaf, lev...]
where the time goes in v4:
time: 47.2 us; the launch traced here: 47.1 us
  Pallas kernels  46.4 us (98%)
  between operations  0.64 us (1%)
    pallas_call x1, Pallas kernels, local(): pl.pallas_call(functools.partial(kernel, (count, leaves, nears, leaf, lev...  45.8 us

profile of v4, /device:TPU:33, one launch (start us, length us, event | category | flops | bytes accessed | tf_op | source)
XLA Modules:
  0.0 47.1 jit_solution(16795208300535958981)
XLA Ops:
  0.6 45.8 %hmatrix.1.out = f32[2,32,128]{2,1,0:T(8,128)S(1)} custom-call(f32[32,128]{1,0:T(8,128)} %bitcast.4, s32[16,11]{1,0:T(8,128)} %ranks_hbm.1, s32[3,16]{1,0:T(4,128)} %bitcast.5, bf16[11,32,4096]{2,1,0:T(8,128)(2,1)} %right_hbm.1, bf16[16,3,256,256]{3,2,1,0:T(8,128)(2,1)} %near_hbm.1, bf16[11,32,4096]{2,1,0:T(8,128)(2,1)} %left_hbm.1), custom_call_target="tpu_custom_call" | custom-call | tf_op jit(solution)/shard_map/hmatrix/pallas_call | solution.py:480
  46.4 0.6 %write.1 = (f32[32,128]{1,0:T(8,128)}, f32[32,128]{1,0:T(8,128)}) custom-call(f32[2,32,128]{2,1,0:T(8,128)S(1)} %hmatrix.1.out), custom_call_target="tpu_custom_call" | custom-call | tf_op jit(solution)/shard_map/write/pallas_call | solution.py:516

commit v5 on v4

--- a/solution.py
+++ b/solution.py
@@ -36,7 +36,7 @@
     shape,
     slip_hbm, ranks_hbm, index_hbm, right_hbm, near_hbm, left_hbm,
     out,
-    slip, ranks, index, right, near, left, own, halo, masks, picks, sums, partial,
+    slip, ranks, index, right, near, left, own, halo, masks, picks, sums, partial, turned,
     mail, got, known, relay, got_relay, plane_sums, got_plane, got_all, got_pair,
     load_sem, piece_sem, halo_send, halo_recv, level_send, level_recv, relay_send, relay_recv,
     plane_send, plane_recv, all_send, all_recv, pair_send, pair_recv, ready, near_ready, plane_ready,
@@ -153,6 +153,31 @@
             scale = jnp.where(lane1 // rank == part, value, scale)
         return scale
 
+    def turn():
+        r = lax.broadcasted_iota(jnp.int32, (leaf, leaf), 0)
+        eye = (r == lax.broadcasted_iota(jnp.int32, (leaf, leaf), 1)).astype(F32).astype(BF16)
+
+        def pair_of(n, carry):
+            for m in range(2):
+                c = n * 2 + m
+                block = right[high:levels, :, pl.ds(pl.multiple_of(c * leaf, leaf), leaf)]
+                turned[c] = dot(eye, block.reshape(leaf, leaf), NT).astype(BF16)
+            return carry
+
+        lax.fori_loop(0, leaves // 2, pair_of, 0)
+
+    def project_turned(vf):
+        @pl.when(spot >= 0)
+        def _():
+            totals = [jnp.zeros((leaves, leaf), F32)] * 2
+            for c in range(leaves):
+                lhs = jnp.where(row == c, vf, 0.0).astype(BF16)
+                totals[c % 2] += dot(lhs, turned[c], NN)
+            for n in range(2):
+                sums[n] = totals[n]
+
+        return sums[0] + sums[1]
+
     def project(vf, start, stop, ready=()):
         rows = (stop - start) * rank
         @pl.when(spot >= 0)
@@ -199,7 +224,7 @@
 
     def write_mail(step, vf, ready=()):
         own[step] = vf.astype(BF16)
-        summed = project(vf, high, levels, ready)
+        summed = project_turned(vf) if step else project(vf, high, levels, ready)
         device_sums = jnp.sum(summed, axis=0, keepdims=True)
         one = pltpu.roll(device_sums[:, :LANES], 2 * rank, 1)
         two = pltpu.roll(device_sums[:, LANES:], 2 * rank, 1)
@@ -293,21 +318,24 @@
     def send_letter(t, sem):
         send(mail.at[0], got.at[t], level_send.at[sem], level_recv.at[sem], jnp.bitwise_xor(me, t))
 
-    for t in reversed(range(1, quad)):
-        send_letter(t, 1)
-    @pl.when(outer)
-    def _():
-        for t in reversed(range(quad, 2 * quad)):
-            send_letter(t, 2)
-
-    for j, first_step, stride, length in runs:
-        if j > quad_bits:
-            @pl.when(bit(j))
-            def _(j=j, first_step=first_step, stride=stride, length=length):
+    def send_down():
+        for j, first_step, stride, length in runs:
+            if j > quad_bits:
                 def both(step):
                     for c in range(2):
                         send_letter(step * 2 + c, 0)
                 run(first_step, stride, length, both)
+
+    @pl.when(outer)
+    def _():
+        pl.when(jnp.logical_not(low))(send_down)
+        for t in reversed(range(quad, 2 * quad)):
+            send_letter(t, 2)
+
+    for t in reversed(range(1, quad)):
+        send_letter(t, 1)
+    pl.when(jnp.logical_and(inner, jnp.logical_not(low)))(send_down)
+
     pl.when(jnp.logical_not(top))(lambda: pl.semaphore_wait(near_ready.at[0], 1))
     send_halo(0, 0)
     pl.when(jnp.logical_not(bottom))(lambda: send_halo(0, 1))
@@ -397,6 +425,7 @@
         pl.when(plane_above(g))(lambda g=g: pl.semaphore_wait(plane_ready.at[g], 1))
         send(plane_sums, got_plane.at[g], plane_send.at[0], plane_recv.at[0], peer_of(g, 0, 0))
     total = apply_ring(got[1, 1], known[2])
+    turn()
     rows_done(got_plane, groups - 1, plane_recv.at[0])
     far_sum = jnp.where(lane1 < rank, got_plane[1], add_all(got_plane[g] for g in range(2, groups)))
     first = apply_far(total, spread(2, far_sum * plane_scale), levels - FAR_BITS, levels)
@@ -410,18 +439,20 @@
         slot = g * plane + step * 2 + c
         send(mail.at[1, sem], got_all.at[slot], all_send.at[sem], all_recv.at[sem], peer_of(g, step, c))
 
-    for j, first_step, stride, length in runs:
-        def all_of(step):
-            for g in far_first:
-                for c in range(2):
-                    send_row(g, step, c)
+    def all_of(step):
+        for g in far_first:
+            for c in range(2):
+                send_row(g, step, c)
+
+    for n, (_, first_step, stride, length) in enumerate(runs):
         run(first_step, stride, length, all_of)
+        if n == 1:
+            send_halo(1, 0)
+            send_halo(1, 1)
     for g in far_first[:-1]:
         for c in range(2):
             send_row(g, 0, c)
     send(mail.at[1, 1], got_pair, pair_send.at[0], pair_recv.at[0], peer_of(0, 0, 1))
-    send_halo(1, 0)
-    send_halo(1, 1)
     local_part(1, vf, last_local)
     pltpu.make_async_copy(got_pair, got_pair, pair_recv.at[0]).wait()
     rows_done(got_all, plane - 2, all_recv.at[0])
@@ -472,6 +503,7 @@
     cross = levels - (leaves.bit_length() - 1)
     ring_bits = cross - FAR_BITS - 1
     plane = count // 2**FAR_BITS
+    assert (levels - leaves.bit_length() + 2) * rank == leaf
     assert leaf == 2 * LANES and 4 * rank == LANES and 2**cross == count
     assert leaves == 16 and ring_bits == 4
     flat = (patches // LANES, LANES)
@@ -495,6 +527,7 @@
             pltpu.VMEM((nears, leaves, leaf), F32),
             pltpu.VMEM((2, leaves, leaf), F32),
             pltpu.VMEM((leaves, leaf), F32),
+            pltpu.VMEM((leaves, leaf, leaf), BF16),
             pltpu.VMEM((2, 2, 1, LANES), F32),
             pltpu.VMEM((plane, 2, 1, LANES), F32),
             pltpu.VMEM((3, 1, LANES), F32),

time: 47.2 us -> 46.9 us (level)
  no operation moved by 1% of the time
where the time goes in v5:
time: 46.9 us; the launch traced here: 46.8 us
  Pallas kernels  46.2 us (99%)
  between operations  0.64 us (1%)
    pallas_call x1, Pallas kernels, local(): pl.pallas_call(functools.partial(kernel, (count, leaves, nears, leaf, lev...  45.5 us

profile of v5, /device:TPU:33, one launch (start us, length us, event | category | flops | bytes accessed | tf_op | source)
XLA Modules:
  0.0 46.8 jit_solution(2836466651187622201)
XLA Ops:
  0.6 45.5 %hmatrix.1.out = f32[2,32,128]{2,1,0:T(8,128)S(1)} custom-call(f32[32,128]{1,0:T(8,128)} %bitcast.4, s32[16,11]{1,0:T(8,128)} %ranks_hbm.1, s32[3,16]{1,0:T(4,128)} %bitcast.5, bf16[11,32,4096]{2,1,0:T(8,128)(2,1)} %right_hbm.1, bf16[16,3,256,256]{3,2,1,0:T(8,128)(2,1)} %near_hbm.1, bf16[11,32,4096]{2,1,0:T(8,128)(2,1)} %left_hbm.1), custom_call_target="tpu_custom_call" | custom-call | tf_op jit(solution)/shard_map/hmatrix/pallas_call | solution.py:512
  46.2 0.6 %write.1 = (f32[32,128]{1,0:T(8,128)}, f32[32,128]{1,0:T(8,128)}) custom-call(f32[2,32,128]{2,1,0:T(8,128)S(1)} %hmatrix.1.out), custom_call_target="tpu_custom_call" | custom-call | tf_op jit(solution)/shard_map/write/pallas_call | solution.py:549

commit v6 on v5

--- a/solution.py
+++ b/solution.py
@@ -13,7 +13,7 @@
 BF16 = jnp.bfloat16
 LANES = 128
 FAR_BITS = 2
-PIECES = 4
+PIECES = 8
 NEAR_UNROLL = 4
 NT = (((1,), (1,)), ((), ()))
 NN = (((1,), (0,)), ((), ()))

time: 46.9 us -> 47 us (level)
  no operation moved by 1% of the time
where the time goes in v6:
time: 47 us; the launch traced here: 46.9 us
  Pallas kernels  46.3 us (99%)
  between operations  0.64 us (1%)
    pallas_call x1, Pallas kernels, local(): pl.pallas_call(functools.partial(kernel, (count, leaves, nears, leaf, lev...  45.6 us

profile of v6, /device:TPU:33, one launch (start us, length us, event | category | flops | bytes accessed | tf_op | source)
XLA Modules:
  0.0 46.9 jit_solution(15368505504826371325)
XLA Ops:
  0.6 45.6 %hmatrix.1.out = f32[2,32,128]{2,1,0:T(8,128)S(1)} custom-call(f32[32,128]{1,0:T(8,128)} %bitcast.4, s32[16,11]{1,0:T(8,128)} %ranks_hbm.1, s32[3,16]{1,0:T(4,128)} %bitcast.5, bf16[11,32,4096]{2,1,0:T(8,128)(2,1)} %right_hbm.1, bf16[16,3,256,256]{3,2,1,0:T(8,128)(2,1)} %near_hbm.1, bf16[11,32,4096]{2,1,0:T(8,128)(2,1)} %left_hbm.1), custom_call_target="tpu_custom_call" | custom-call | tf_op jit(solution)/shard_map/hmatrix/pallas_call | solution.py:512
  46.3 0.6 %write.1 = (f32[32,128]{1,0:T(8,128)}, f32[32,128]{1,0:T(8,128)}) custom-call(f32[2,32,128]{2,1,0:T(8,128)S(1)} %hmatrix.1.out), custom_call_target="tpu_custom_call" | custom-call | tf_op jit(solution)/shard_map/write/pallas_call | solution.py:549
